TPU v7x, 256 devices: a whole 4x4x8 slice. The times are simulated.
256 devices in a mesh: seq: 16 (over y, x), grp: 16 (over z, core).
Axes of the slice: x: 4, y: 4, z: 8, core: 2. Of those that a mesh axis runs over, the one named last changes fastest.
Arguments:
- conv_input: bfloat16 [16, 8192, 5120], P('grp', 'seq'), may hold values from -6 to 6
- step_raw: float32 [16, 64, 8192], P('grp', None, 'seq'), may hold values from -5 to 0
- decay_rate: float32 [64], replicated, may hold values from 0 to 2, as said below
- conv_weight: bfloat16 [4, 5120], replicated, may hold values from -3 to 3
- conv_bias: bfloat16 [5120], replicated, may hold values from -3 to 3
- norm_gain: float32 [4096], replicated, may hold values from 0.5 to 1.5
- owner_slot: int32 [16], replicated, may hold values from 0 to 15, each once
Outputs:
- mixed: bfloat16 [16, 8192, 4096], P('grp', 'seq')
- final_ssm: float32 [16, 64, 64, 128], P('seq', 'grp')
- final_conv: bfloat16 [16, 5120, 4], P('seq', 'grp')
Inputs may be any that keep to these rules, and one draw needn't show every extreme that they name: `decay_rate`: positive. `owner_slot`: every decode row receives exactly one prompt.
All inputs are finite; a program needn't handle non-finite values.
Results may differ from a plain program's by a relative error of at most 0.009.
Values may be sent and summed in bfloat16 or wider, within the bound.
No kernel may reach another device: no remote copies, remote signals or barrier semaphores. Data moves between devices by JAX's collectives and lax.ppermute only.
A program may use at most 128 MiB of HBM per device.

v0:
```python
import math

import jax
import jax.numpy as jnp
from jax import lax
from jax.sharding import Mesh
from jax.sharding import PartitionSpec as P

HEADS = 64
HEAD_DIM = 64
STATE = 128
GROUPS = 4
BLOCK = 256
D_IN = 4096
SEQ = ("seq_0", "seq_1")


NORM_EPS = 1.0


def passed_along(block, axis, distance):
    devices = range(lax.axis_size(axis))
    route = [(i - distance, i) for i in devices if i - distance in devices]
    return lax.ppermute(block, axis, route)


def filled_with(shard, identity):
    return jax.tree.map(
        lambda a, e: jnp.broadcast_to(jnp.asarray(e, a.dtype), a.shape), shard, identity
    )


def entering(shard, axes, combine, identity):
    before = start = filled_with(shard, identity)
    subtotal = shard
    for axis in reversed(axes):
        length, mine = (lax.axis_size(axis), lax.axis_index(axis))
        pieces = jax.tree.map(lambda part: lax.all_gather(part, axis), subtotal)
        inside, subtotal = (start, start)
        for k in range(length):
            passed = k < mine
            subtotal = combine(subtotal, jax.tree.map(lambda part: part[k], pieces))
            inside = jax.tree.map(lambda new, old: jnp.where(passed, new, old), subtotal, inside)
        before = combine(inside, before)
    return before


def laid_out(pieces, dim):
    pieces = jnp.moveaxis(pieces, 0, dim)
    lengths = pieces.shape
    return pieces.reshape(*lengths[:dim], lengths[dim] * lengths[dim + 1], *lengths[dim + 2 :])


def from_everyone(shard, axis):
    copies = jnp.broadcast_to(shard, (lax.axis_size(axis), *shard.shape))
    return lax.all_to_all(copies, axis, split_axis=0, concat_axis=0, tiled=True)


def gathered_copies(shard, axis, dim):
    return laid_out(from_everyone(shard, axis), dim)


def in_blocks(shard, dim, length):
    lengths = shard.shape
    pieces = shard.reshape(*lengths[:dim], length, lengths[dim] // length, *lengths[dim + 1 :])
    return jnp.moveaxis(pieces, dim, 0)


def piece_ends(length, count):
    turn = length // count
    if turn >= 8:
        turn -= turn % 8
    return [turn * k for k in range(1, count)]


def several_exchanges(shard, axis, pieces, split_dim, concat_dim):
    blocks = in_blocks(shard, split_dim, lax.axis_size(axis))
    split_at = max(range(1, max(2, blocks.ndim - 1)), key=lambda d: blocks.shape[d])
    gathered = []
    for share in jnp.split(blocks, piece_ends(blocks.shape[split_at], pieces), axis=split_at):
        if share.size:
            gathered.append(lax.all_to_all(share, axis, split_axis=0, concat_axis=0, tiled=True))
    return laid_out(jnp.concatenate(gathered, axis=split_at), concat_dim)


def sent_and_summed(shard, axis, dim):
    length = lax.axis_size(axis)
    pieces = lax.all_to_all(in_blocks(shard, dim, length), axis, 0, 0, tiled=True)
    return jnp.sum(pieces.astype(jnp.float32), axis=0)


def sent_together(arrays, axis, dim, along):
    widths = [math.prod(a.shape[along:]) for a in arrays]
    both = jnp.concatenate(
        [a.reshape(*a.shape[:along], w) for a, w in zip(arrays, widths)], axis=along
    )
    out = sent_and_summed(both, axis, dim)
    pieces = jnp.split(out, [sum(widths[:k]) for k in range(1, len(widths))], axis=along)
    return tuple((b.reshape(*out.shape[:along], *a.shape[along:]) for a, b in zip(arrays, pieces)))


def conv_silu(padded, conv_weight, conv_bias):
    width = conv_weight.shape[0]
    length = padded.shape[0] - width + 1
    total = (
        jnp.zeros((length, padded.shape[1]), jnp.float32) + conv_bias.astype(jnp.float32)[None, :]
    )
    for offset in range(width):
        total = total + conv_weight[offset].astype(jnp.float32)[None, :] * padded[
            offset : offset + length
        ].astype(jnp.float32)
    return jax.nn.silu(total).astype(jnp.bfloat16)


def block_terms(inputs, b_matrix, c_matrix, step_size, log_decay):
    width = log_decay.shape[-1]
    summed = jnp.cumsum(log_decay, axis=-1)
    scores = jnp.einsum("tgn,ugn->gtu", c_matrix, b_matrix, preferred_element_type=jnp.float32)
    causal = jnp.arange(width)[:, None] >= jnp.arange(width)[None, :]
    spread = jnp.exp(jnp.minimum(summed[:, :, :, None] - summed[:, :, None, :], 0.0))
    weights = (
        jnp.where(causal, spread, 0.0) * step_size[:, :, None, :] * scores[:, None, :, :]
    ).astype(jnp.bfloat16)
    intra = jnp.einsum("gktu,ugkp->tgkp", weights, inputs, preferred_element_type=jnp.float32)
    tail = jnp.exp(summed[:, :, -1:] - summed) * step_size
    scaled = (
        tail[..., None] * jnp.swapaxes(b_matrix, 0, 1).astype(jnp.float32)[:, None, :, :]
    ).astype(jnp.bfloat16)
    local = jnp.einsum("gkun,ugkp->gkpn", scaled, inputs, preferred_element_type=jnp.float32)
    return (intra, local, jnp.exp(summed[:, :, -1]), jnp.exp(summed))


def from_state(c_matrix, carried, scale):
    reach = jnp.einsum(
        "tgn,gkpn->tgkp", c_matrix, carried.astype(jnp.bfloat16), preferred_element_type=jnp.float32
    )
    return reach * jnp.transpose(scale, (2, 0, 1))[..., None]


def chain_combine(earlier, later):
    return (earlier[0] * later[0], later[0][:, :, None, None] * earlier[1] + later[1])


def body(conv_input, step_raw, decay_rate, conv_weight, conv_bias, norm_gain, owner_slot):
    width = conv_weight.shape[0]
    own_rows = conv_input[0]
    length = own_rows.shape[0]
    before = passed_along(conv_input[:, length - width + 1 :, :], SEQ, 1)
    padded = jnp.concatenate([before[0], own_rows], axis=0)
    conved = conv_silu(padded, conv_weight, conv_bias)
    blocks = length // BLOCK
    per_group = HEADS // GROUPS
    inputs = conved[:, :D_IN].reshape(blocks, BLOCK, GROUPS, per_group, HEAD_DIM)
    b_matrix = conved[:, D_IN : D_IN + GROUPS * STATE].reshape(blocks, BLOCK, GROUPS, STATE)
    c_matrix = conved[:, D_IN + GROUPS * STATE :].reshape(blocks, BLOCK, GROUPS, STATE)
    step_size = jax.nn.softplus(step_raw[0])
    log_decay = -step_size * decay_rate[:, None]
    shard_log = jnp.sum(log_decay, axis=-1).reshape(GROUPS, per_group)
    step_size = step_size.reshape(GROUPS, per_group, blocks, BLOCK)
    log_decay = log_decay.reshape(GROUPS, per_group, blocks, BLOCK)
    pieces = []
    end_state = jnp.zeros((GROUPS, per_group, HEAD_DIM, STATE), jnp.float32)
    for number in range(blocks):
        terms = block_terms(
            inputs[number],
            b_matrix[number],
            c_matrix[number],
            step_size[:, :, number],
            log_decay[:, :, number],
        )
        pieces.append(terms)
        end_state = terms[2][:, :, None, None] * end_state + terms[1]
    shard_decay = jnp.exp(shard_log)
    identity = (jnp.ones_like(shard_decay), jnp.zeros_like(end_state))
    scanned = entering((shard_decay, end_state), SEQ, chain_combine, identity)
    incoming = scanned[1]
    carried = incoming
    outputs = []
    for number in range(blocks):
        intra, local, decay, scale = pieces[number]
        outputs.append(intra + from_state(c_matrix[number], carried, scale))
        carried = decay[:, :, None, None] * carried + local
    values = jnp.concatenate(outputs, axis=0).reshape(length, GROUPS, per_group * HEAD_DIM)
    norm_scale = lax.rsqrt(jnp.mean(values * values, axis=-1) + NORM_EPS)
    mixed = ((values * norm_scale[..., None]).reshape(length, D_IN) * norm_gain[None, :]).astype(
        jnp.bfloat16
    )[None]
    place = lax.axis_index(SEQ)
    last = lax.axis_size(SEQ) - 1
    kept = jnp.transpose(own_rows[length - width :], (1, 0)).astype(jnp.float32)[None]
    shard_logs = gathered_copies(shard_log[None], SEQ, 0)
    after = jnp.arange(shard_logs.shape[0]) > place
    later_log = jnp.sum(jnp.where(after[:, None, None], shard_logs, 0.0), axis=0)
    sent_state = (jnp.exp(later_log)[:, :, None, None] * end_state).reshape(
        1, HEADS, HEAD_DIM, STATE
    )
    sent_conv = jnp.where(place == last, kept, 0.0)
    got_state, got_conv = (
        several_exchanges(sent_state, "grp", 2, 1, 0),
        several_exchanges(sent_conv, "grp", 2, 1, 0),
    )
    placed_state = jnp.zeros_like(got_state).at[owner_slot].set(got_state)
    placed_conv = jnp.zeros_like(got_conv).at[owner_slot].set(got_conv)
    final_ssm, summed_conv = sent_together(
        (placed_state.astype(jnp.bfloat16), placed_conv.astype(jnp.bfloat16)), SEQ, 0, 1
    )
    final_conv = summed_conv.astype(jnp.bfloat16)
    return (mixed, final_ssm, final_conv)


def solution(mesh):
    torus = Mesh(mesh.devices.reshape(4, 4, mesh.shape["grp"]), ("seq_0", "seq_1", "grp"))
    return jax.shard_map(
        body,
        mesh=torus,
        in_specs=(P("grp", SEQ, None), P("grp", None, SEQ), P(), P(), P(), P(), P()),
        out_specs=(P("grp", SEQ, None), P(SEQ, "grp", None, None), P(SEQ, "grp", None)),
        check_vma=False,
    )
```

profile of v0, /device:TPU:1, one launch (start us, length us, event | category | flops | bytes accessed | tf_op | source)
XLA Modules:
  0.0 367.4 jit_solution(10572802933433731296)
XLA Ops:
  7.2 1.1 fusion.40
  8.3 0.6 broadcast_in_dim.36
  9.0 7.6 %all-to-all-start = ((f32[16,1,4,16]{3,2,1,0:T(4,128)}), f32[16,1,4,16]{3,2,1,0:T(4,128)S(1)}, u32[]{:S(2)}, u32[]{:S(2)}) async-start(f32[16,1,4,16]{3,2,1,0:T(4,128)} %broadcast_in_dim.36), calls=%async_computation | async-start | bytes 65536 | tf_op jit(solution)/shard_map/all_to_all | solution.py:56
  16.6 0.9 slice.144
  17.5 3.3 collective-permute-start
  20.8 0.7 mul.381
  21.5 1.0 squeeze.86
  22.5 1.0 slice_convert_fusion.3
  24.1 2.3 reduce-window.14
  26.4 2.3 reduce-window.16
  29.0 0.6 copy-done.17
  30.9 0.7 exponential_bitcast_fusion.1
  31.6 0.7 exponential_bitcast_fusion
  32.4 7.9 %copy.128 = bf16[1,512,5120]{1,2,0:T(8,128)(2,1)} copy(bf16[1,512,5120]{2,1,0:T(8,128)(2,1)} %param.7) | data formatting | bytes 10485760 | tf_op args[0]
  40.4 0.6 copy.127
  41.1 18.3 %multiply_convert_fusion.2 = bf16[512,5120]{0,1:T(8,128)(2,1)S(1)} fusion(bf16[512,5120]{0,1:T(8,128)(2,1)} %bitcast.215, bf16[3,5120]{0,1:T(8,128)(2,1)S(1)} %bitcast.219, f32[5120]{0:T(1024)S(1)} %bitcast.238, f32[5120]{0:T(1024)S(1)} %bitcast.239, f32[5120]{0:T(1024)S(1)} %bitcast.237, f32[5120]{0:T(1024)S(1)} %bitcast.236, f32[5120]{0:T(1024)S(1)} %convert_element_type.92), kind=kLoop, calls=%fused_computation.4 | loop fusion | flops 68157440 | bytes 10618880 | tf_op jit(solution)/shard_map/convert_element_type | solution.py:112
  59.4 0.8 fusion.57
  60.2 2.3 fusion.58
  63.0 4.7 %fusion.16 = f32[4,16,64,128]{3,2,1,0:T(8,128)S(1)} fusion(bf16[256,4,16,64]{0,3,2,1:T(8,128)(2,1)} %bitcast.230, f32[4,256,128]{2,1,0:T(8,128)S(1)} %copy.139, f32[4,16,256]{2,1,0:T(8,128)S(1)} %get-tuple-element.37), kind=kOutput, calls=%fused_computation.31 | convolution fusion | flops 272629760 | bytes 4784128 | tf_op jit(solution)/shard_map/gkun,ugkp->gkpn/dot_general | solution.py:129
  67.7 5.6 %broadcast_multiply_fusion = (f32[4,16,64,128]{3,2,1,0:T(8,128)S(1)}, f32[4,16,64,128]{3,2,1,0:T(8,128)}) fusion(f32[4,16]{1,0:T(4,128)S(1)} %exp.85, bf16[256,4,16,64]{0,3,2,1:T(8,128)(2,1)S(1)} %bitcast.217, f32[4,256,128]{2,1,0:T(8,128)S(1)} %copy.140, f32[4,16,256]{2,1,0:T(8,128)S(1)} %get-tuple-element.39, f32[4,16,64,128]{3,2,1,0:T(8,128)S(1)} %fusion.16, ...), kind=kOutput, calls=%fused_computation.66 | convolution fusion | flops 274726912 | bytes 8979200 | tf_op jit(solution)/shard_map/gkun,ugkp->gkpn/dot_general | solution.py:129
  73.5 8.1 %all_gather.18 = f32[4,4,16]{2,1,0:T(4,128)S(1)} all-gather(f32[1,4,16]{2,1,0:T(4,128)S(1)} %exp.77), channel_id=1, replica_groups=mesh['seq_0'=4,'seq_1'=4,'grp'=16] {'seq_1'}, dimensions={0}, use_global_device_ids=true | all-gather | bytes 1280 | tf_op jit(solution)/shard_map/all_gather | solution.py:38
  82.2 79.9 %all-gather.6.cloned.1.call-done = f32[16,16,64,128]{3,2,1,0:T(8,128)} async-done(((f32[4,16,64,128]{3,2,1,0:T(8,128)}), f32[16,16,64,128]{3,2,1,0:T(8,128)}) %all-gather.6.cloned.1.call-update) | async-done | bytes 8388624 | tf_op jit(solution)/shard_map/all_gather | solution.py:38
  162.2 4.8 %bitcast_add_fusion = f32[1,4,16,64,128]{4,3,2,1,0:T(8,128)} fusion(f32[16,16,64,128]{3,2,1,0:T(8,128)} %all-gather.6.cloned.1.call-done, f32[4,16]{1,0:T(4,128)S(1)} %get-tuple-element.45, f32[4,16]{1,0:T(4,128)S(1)} %get-tuple-element.53, f32[4,16]{1,0:T(4,128)S(1)} %get-tuple-element.52, f32[4,16]{1,0:T(4,128)S(1)} %get-tuple-element.51), kind=kLoop, calls=%fused_computation.54 | loop fusion | flops 3670016 | bytes 10486784 | tf_op jit(solution)/shard_map/add | solution.py:141
  167.0 0.9 select_bitcast_fusion
  168.1 0.7 copy.149
  168.8 7.9 %all-to-all-start.3 = ((f32[16,1,160,4]{2,3,1,0:T(4,128)}), f32[16,1,160,4]{2,3,1,0:T(4,128)S(1)}, u32[]{:S(2)}, u32[]{:S(2)}) async-start(f32[16,1,160,4]{2,3,1,0:T(4,128)} %copy.149), calls=%async_computation.3 | async-start | bytes 131072 | tf_op jit(solution)/shard_map/all_to_all | solution.py:82
  176.6 0.7 copy.150
  177.3 7.1 %all-to-all-done.3 = f32[16,1,160,4]{2,3,1,0:T(4,128)S(1)} async-done(((f32[16,1,160,4]{2,3,1,0:T(4,128)}), f32[16,1,160,4]{2,3,1,0:T(4,128)S(1)}, u32[]{:S(2)}, u32[]{:S(2)}) %all-to-all-start.3) | async-done | bytes 40992 | tf_op jit(solution)/shard_map/all_to_all | solution.py:82
  184.4 4.0 %all-to-all-start.4 = ((f32[16,1,160,4]{2,3,1,0:T(4,128)}), f32[16,1,160,4]{2,3,1,0:T(4,128)}, u32[]{:S(2)}, u32[]{:S(2)}) async-start(f32[16,1,160,4]{2,3,1,0:T(4,128)} %copy.150), calls=%async_computation.4 | async-start | bytes 131072 | tf_op jit(solution)/shard_map/all_to_all | solution.py:82
  188.4 1.1 fusion.59
  189.6 6.7 %all-to-all-done.4 = f32[16,1,160,4]{2,3,1,0:T(4,128)} async-done(((f32[16,1,160,4]{2,3,1,0:T(4,128)}), f32[16,1,160,4]{2,3,1,0:T(4,128)}, u32[]{:S(2)}, u32[]{:S(2)}) %all-to-all-start.4) | async-done | bytes 40992 | tf_op jit(solution)/shard_map/all_to_all | solution.py:82
  196.3 31.1 %all_to_all.30 = f32[16,1,4,32,128]{4,3,2,1,0:T(8,128)S(1)} all-to-all(f32[16,1,4,32,128]{4,3,2,1,0:T(8,128)S(1)} %get-tuple-element.28), channel_id=1, replica_groups=mesh['seq_0'=4,'seq_1'=4,'grp'=16] {'grp'}, dimensions={0} | all-to-all | bytes 2097152 | tf_op jit(solution)/shard_map/all_to_all | solution.py:82
  227.5 3.6 all-to-all-start.2
  231.0 0.9 maximum_bitcast_fusion.2
  232.0 1.0 scatter_fusion.1
  233.5 24.9 %all-to-all-done.2 = f32[16,1,4,32,128]{4,3,2,1,0:T(8,128)S(1)} async-done(((f32[16,1,4,32,128]{4,3,2,1,0:T(8,128)}), f32[16,1,4,32,128]{4,3,2,1,0:T(8,128)S(1)}, u32[]{:S(2)}, u32[]{:S(2)}) %all-to-all-start.2) | async-done | bytes 1048608 | tf_op jit(solution)/shard_map/all_to_all | solution.py:82
  258.3 1.6 maximum_bitcast_fusion
  260.1 2.7 scatter_fusion
  263.0 0.7 copy.187
  264.4 1.5 reduce.8
  266.0 1.2 reshape.348
  267.1 6.2 %all-to-all-start.5 = ((bf16[16,2,17024]{2,1,0:T(2,128)(2,1)}), bf16[16,2,17024]{2,1,0:T(2,128)(2,1)S(1)}, u32[]{:S(2)}, u32[]{:S(2)}) async-start(bf16[16,2,17024]{2,1,0:T(2,128)(2,1)} %reshape.348), calls=%async_computation.5 | async-start | bytes 2179072 | tf_op jit(solution)/shard_map/all_to_all | solution.py:88
  273.4 0.6 copy.188
  274.0 0.6 copy.189
  274.6 16.0 %all_gather.19 = f32[4,4,16]{2,1,0:T(4,128)S(1)} all-gather(f32[1,4,16]{2,1,0:T(4,128)S(1)} %copy-done.28), channel_id=1, replica_groups=mesh['seq_0'=4,'seq_1'=4,'grp'=16] {'seq_0'}, dimensions={0}, use_global_device_ids=true | all-gather | bytes 1280 | tf_op jit(solution)/shard_map/all_gather | solution.py:38
  290.6 0.6 iota_compare_fusion
  291.9 1.4 fusion.65
  293.3 1.4 fusion.64
  294.7 2.0 reshape.349
  296.8 2.5 convert_reduce_fusion
  299.4 0.7 split.29
  300.3 0.7 copy.154
  300.9 7.3 %fusion.27 = f32[4,16,64,128]{3,2,1,0:T(8,128)S(1)} fusion(f32[4,4,16,64,128]{4,3,2,1,0:T(8,128)} %all-gather.4.cloned.1.call-done, f32[16,16,64,128]{3,2,1,0:T(8,128)} %all-gather.6.cloned.1.call-done, f32[4,16]{1,0:T(4,128)S(1)} %get-tuple-element.45, f32[4,16]{1,0:T(4,128)S(1)} %get-tuple-element.53, f32[4,16]{1,0:T(4,128)S(1)} %get-tuple-element.52, ...), kind=kLoop, calls=%fused_computation.46 | loop fusion | flops 12582912 | bytes 18876680 | tf_op jit(solution)/shard_map/add | solution.py:141
  308.3 0.7 fusion.36
  309.0 0.9 copy-done.1
  309.9 0.8 fusion.34
  310.7 0.8 copy-done.3
  311.8 5.2 %fusion.18 = f32[256,4,16,64]{0,3,2,1:T(8,128)S(1)} fusion(f32[4,16,64,256]{3,2,1,0:T(8,128)S(1)} %fusion.34, bf16[256,4,16,64]{0,3,2,1:T(8,128)(2,1)S(1)} %bitcast.218, f32[4,256,256]{2,1,0:T(8,128)S(1)} %copy-done.12, f32[4,16,256]{2,1,0:T(8,128)S(1)} %bitcast.241, f32[4,16,256]{2,1,0:T(8,128)S(1)} %copy-done.18, pred[256,256]{1,0:T(8,128)(4,1)S(1)} %copy-done.22, ...), kind=kOutput, calls=%fused_computation.34 | convolution fusion | flops 564133888 | bytes 11796480 | tf_op jit(solution)/shard_map/gktu,ugkp->tgkp/dot_general | solution.py:124
  317.0 5.2 %fusion.19 = f32[256,4,16,64]{0,3,2,1:T(8,128)S(1)} fusion(f32[4,16,64,256]{3,2,1,0:T(8,128)S(1)} %fusion.36, bf16[256,4,16,64]{0,3,2,1:T(8,128)(2,1)S(1)} %bitcast.231, f32[4,256,256]{2,1,0:T(8,128)S(1)} %copy-done.11, f32[4,16,256]{2,1,0:T(8,128)S(1)} %bitcast.240, f32[4,16,256]{2,1,0:T(8,128)S(1)} %copy-done.20, pred[256,256]{1,0:T(8,128)(4,1)S(1)} %copy-done.22, ...), kind=kOutput, calls=%fused_computation.36 | convolution fusion | flops 564133888 | bytes 11796480 | tf_op jit(solution)/shard_map/gktu,ugkp->tgkp/dot_general | solution.py:124
  322.2 3.9 %multiply_reduce_fusion = (f32[512,4]{0,1:T(4,128)S(1)}, f32[512,4,16,64]{0,3,2,1:T(8,128)}) fusion(f32[256,4,16,64]{0,3,2,1:T(8,128)S(1)} %fusion.18, f32[256,4,16,64]{0,3,2,1:T(8,128)S(1)} %fusion.19), kind=kLoop, calls=%fused_computation.11 | loop fusion | flops 6289408 | bytes 16785408 | tf_op jit(solution)/shard_map/reduce_sum | solution.py:184
  326.1 9.2 %copy.146 = f32[1,512,4096]{2,1,0:T(8,128)} copy(f32[1,512,4096]{1,2,0:T(8,128)} %bitcast.214) | data formatting | bytes 16777216 | tf_op jit(solution)/shard_map/reshape | solution.py:183
  335.5 4.4 %mul.449 = f32[512,4,1024]{2,1,0:T(4,128)} broadcast(f32[512,4]{1,0:T(8,128)S(1)} %copy.145), dimensions={0,1} | broadcast | bytes 8396800 | tf_op jit(solution)/shard_map/mul | solution.py:185
  339.9 10.9 %mul.450 = f32[1,512,4096]{2,1,0:T(8,128)} reshape(f32[512,4,1024]{2,1,0:T(4,128)} %mul.449) | data formatting | bytes 16777216 | tf_op jit(solution)/shard_map/mul | solution.py:185
  350.7 9.8 %multiply_convert_fusion.5 = bf16[1,512,4096]{2,1,0:T(8,128)(2,1)} fusion(f32[1,512,4096]{2,1,0:T(8,128)} %copy.146, f32[1,512,4096]{2,1,0:T(8,128)} %mul.450, f32[4096]{0:T(1024)S(1)} %copy-done.26), kind=kLoop, calls=%fused_computation.10 | loop fusion | flops 6291456 | bytes 20987904 | tf_op jit(solution)/shard_map/convert_element_type | solution.py:185
  (115 shorter events, 6.7 us)
Async XLA Ops:
  9.0 31.3 %all-to-all-start = ((f32[16,1,4,16]{3,2,1,0:T(4,128)}), f32[16,1,4,16]{3,2,1,0:T(4,128)S(1)}, u32[]{:S(2)}, u32[]{:S(2)}) async-start(f32[16,1,4,16]{3,2,1,0:T(4,128)} %broadcast_in_dim.36), calls=%async_computation | async-start | bytes 65536 | tf_op jit(solution)/shard_map/all_to_all | solution.py:56
  16.6 145.6 %all-gather.6.cloned.1.call-start = ((), (), s32[]{:S(2)}) async-start(), calls=%async_computation.7 | async-start | bytes 10485760 | tf_op jit(solution)/shard_map/all_gather | solution.py:38
  17.5 22.9 %collective-permute-start = (bf16[1,3,5120]{2,1,0:T(4,128)(2,1)S(1)}, bf16[1,3,5120]{2,1,0:T(4,128)(2,1)S(1)}, u32[]{:S(2)}, u32[]{:S(2)}) collective-permute-start(bf16[1,3,5120]{2,1,0:T(4,128)(2,1)S(1)} %slice.144), channel_id=1, source_target_pairs={{0,16},{16,32},{32,48},{48,64},{64,80},{80,96},{96,112},{112,128},... | collective-permute-start | bytes 92168 | tf_op jit(solution)/shard_map/ppermute | solution.py:24
  24.1 16.2 %copy-start.13 = (f32[4,16,1,256]{3,2,1,0:T(1,128)}, f32[4,16,1,256]{3,2,1,0:T(1,128)S(1)}, u32[]{:S(2)}) copy-start(f32[4,16,1,256]{3,2,1,0:T(1,128)S(1)} %get-tuple-element.31) | copy-start | bytes 196612
  24.1 16.2 %copy-start.15 = (f32[4,16,1,256]{3,2,1,0:T(1,128)}, f32[4,16,1,256]{3,2,1,0:T(1,128)S(1)}, u32[]{:S(2)}) copy-start(f32[4,16,1,256]{3,2,1,0:T(1,128)S(1)} %get-tuple-element.30) | copy-start | bytes 196612
  29.0 0.6 copy-start.17
  30.1 0.6 copy-start.19
  32.3 8.0 %copy-start.27 = (bf16[5120]{0:T(1024)(128)(2,1)S(1)}, bf16[5120]{0:T(1024)(128)(2,1)}, u32[]{:S(2)}) copy-start(bf16[5120]{0:T(1024)(128)(2,1)} %param.11) | copy-start | bytes 30724
  60.2 2.3 copy-start.6
  60.2 2.6 copy-start.8
  63.0 4.8 %copy-start.2 = (bf16[256,4096]{0,1:T(8,128)(2,1)S(1)}, bf16[256,4096]{0,1:T(8,128)(2,1)}, u32[]{:S(2)}) copy-start(bf16[256,4096]{0,1:T(8,128)(2,1)} %get-tuple-element.26) | copy-start | bytes 6291460
  67.7 5.6 %copy-start = (f32[4,16,64,128]{3,2,1,0:T(8,128)}, f32[4,16,64,128]{3,2,1,0:T(8,128)S(1)}, u32[]{:S(2)}) copy-start(f32[4,16,64,128]{3,2,1,0:T(8,128)S(1)} %fusion.16) | copy-start | bytes 6291460
  73.4 227.6 %all-gather.4.cloned.1.call-start = ((), (), s32[]{:S(2)}) async-start(), calls=%async_computation.6 | async-start | bytes 10485760 | tf_op jit(solution)/shard_map/all_gather | solution.py:38
  168.8 15.6 %all-to-all-start.3 = ((f32[16,1,160,4]{2,3,1,0:T(4,128)}), f32[16,1,160,4]{2,3,1,0:T(4,128)S(1)}, u32[]{:S(2)}, u32[]{:S(2)}) async-start(f32[16,1,160,4]{2,3,1,0:T(4,128)} %copy.149), calls=%async_computation.3 | async-start | bytes 131072 | tf_op jit(solution)/shard_map/all_to_all | solution.py:82
  184.4 11.9 %all-to-all-start.4 = ((f32[16,1,160,4]{2,3,1,0:T(4,128)}), f32[16,1,160,4]{2,3,1,0:T(4,128)}, u32[]{:S(2)}, u32[]{:S(2)}) async-start(f32[16,1,160,4]{2,3,1,0:T(4,128)} %copy.150), calls=%async_computation.4 | async-start | bytes 131072 | tf_op jit(solution)/shard_map/all_to_all | solution.py:82
  189.6 41.4 %copy-start.29 = (s32[16]{0:T(128)S(1)}, s32[16]{0:T(128)}, u32[]{:S(2)}) copy-start(s32[16]{0:T(128)} %param.13) | copy-start | bytes 196
  227.5 30.9 %all-to-all-start.2 = ((f32[16,1,4,32,128]{4,3,2,1,0:T(8,128)}), f32[16,1,4,32,128]{4,3,2,1,0:T(8,128)S(1)}, u32[]{:S(2)}, u32[]{:S(2)}) async-start(f32[16,1,4,32,128]{4,3,2,1,0:T(8,128)} %get-tuple-element.29), calls=%async_computation.2 | async-start | bytes 2097152 | tf_op jit(solution)/shard_map/all_to_all | solution.py:82
  265.9 7.5 %copy-start.16 = (f32[4,16,1,256]{3,2,1,0:T(1,128)S(1)}, f32[4,16,1,256]{3,2,1,0:T(1,128)}, u32[]{:S(2)}) copy-start(f32[4,16,1,256]{3,2,1,0:T(1,128)} %copy-done.15) | copy-start | bytes 196612
  265.9 8.1 %copy-start.14 = (f32[4,16,1,256]{3,2,1,0:T(1,128)S(1)}, f32[4,16,1,256]{3,2,1,0:T(1,128)}, u32[]{:S(2)}) copy-start(f32[4,16,1,256]{3,2,1,0:T(1,128)} %copy-done.13) | copy-start | bytes 196612
  265.9 8.7 %copy-start.28 = (f32[1,4,16]{2,1,0:T(4,128)S(1)}, f32[1,4,16]{2,1,0:T(4,128)}, u32[]{:S(2)}) copy-start(f32[1,4,16]{2,1,0:T(4,128)} %get-tuple-element.50) | copy-start | bytes 772
  265.9 25.9 %copy-start.9 = (bf16[256,512]{0,1:T(8,128)(2,1)S(1)}, bf16[256,512]{0,1:T(8,128)(2,1)}, u32[]{:S(2)}) copy-start(bf16[256,512]{0,1:T(8,128)(2,1)} %copy-done.8) | copy-start | bytes 786436
  265.9 27.3 %copy-start.4 = (bf16[256,512]{0,1:T(8,128)(2,1)S(1)}, bf16[256,512]{0,1:T(8,128)(2,1)}, u32[]{:S(2)}) copy-start(bf16[256,512]{0,1:T(8,128)(2,1)} %get-tuple-element.22) | copy-start | bytes 786436
  266.0 27.3 %copy-start.7 = (bf16[256,512]{0,1:T(8,128)(2,1)S(1)}, bf16[256,512]{0,1:T(8,128)(2,1)}, u32[]{:S(2)}) copy-start(bf16[256,512]{0,1:T(8,128)(2,1)} %copy-done.6) | copy-start | bytes 786436
  267.1 27.6 %all-to-all-start.5 = ((bf16[16,2,17024]{2,1,0:T(2,128)(2,1)}), bf16[16,2,17024]{2,1,0:T(2,128)(2,1)S(1)}, u32[]{:S(2)}, u32[]{:S(2)}) async-start(bf16[16,2,17024]{2,1,0:T(2,128)(2,1)} %reshape.348), calls=%async_computation.5 | async-start | bytes 2179072 | tf_op jit(solution)/shard_map/all_to_all | solution.py:88
  300.9 7.3 %copy-start.5 = (bf16[256,512]{0,1:T(8,128)(2,1)S(1)}, bf16[256,512]{0,1:T(8,128)(2,1)}, u32[]{:S(2)}) copy-start(bf16[256,512]{0,1:T(8,128)(2,1)} %get-tuple-element.22) | copy-start | bytes 786436
  308.3 1.6 copy-start.1
  309.9 1.6 copy-start.3
  309.9 1.9 copy-start.12
  309.9 1.9 copy-start.18
  309.9 1.9 copy-start.22
  309.9 1.9 copy-start.23
  309.9 1.9 copy-start.25
  311.8 5.2 %copy-start.10 = (bf16[256,4096]{0,1:T(8,128)(2,1)S(1)}, bf16[256,4096]{0,1:T(8,128)(2,1)}, u32[]{:S(2)}) copy-start(bf16[256,4096]{0,1:T(8,128)(2,1)} %get-tuple-element.27) | copy-start | bytes 6291460
  311.8 5.2 %copy-start.11 = (f32[4,256,256]{2,1,0:T(8,128)S(1)}, f32[4,256,256]{2,1,0:T(8,128)}, u32[]{:S(2)}) copy-start(f32[4,256,256]{2,1,0:T(8,128)} %fusion.64) | copy-start | bytes 3145732
  311.8 5.2 %copy-start.20 = (f32[4,16,256]{2,1,0:T(8,128)S(1)}, f32[4,16,256]{2,1,0:T(8,128)}, u32[]{:S(2)}) copy-start(f32[4,16,256]{2,1,0:T(8,128)} %copy-done.19) | copy-start | bytes 196612
  311.8 5.2 %copy-start.21 = (f32[4,16,1,256]{3,1,2,0:T(8,128)S(1)}, f32[4,16,1,256]{3,1,2,0:T(8,128)}, u32[]{:S(2)}) copy-start(f32[4,16,1,256]{3,1,2,0:T(8,128)} %copy.189) | copy-start | bytes 196612
  311.8 5.2 %copy-start.24 = (f32[256,4,16]{0,2,1:T(8,128)S(1)}, f32[256,4,16]{0,2,1:T(8,128)}, u32[]{:S(2)}) copy-start(f32[256,4,16]{0,2,1:T(8,128)} %get-tuple-element.36) | copy-start | bytes 196612
  339.9 10.9 %copy-start.26 = (f32[4096]{0:T(1024)S(1)}, f32[4096]{0:T(1024)}, u32[]{:S(2)}) copy-start(f32[4096]{0:T(1024)} %param.12) | copy-start | bytes 49156
Sparse Core Ops, SparseCore 0:
  73.5 88.6 all-gather.5
  167.1 86.6 all-gather.3
where the time goes:
time: 370 us; the launch traced here: 367 us
  waiting for transfers between devices  119 us (32%)
  other arithmetic  62.5 us (17%)
  local copies, waits for them, and re-layouts  58.7 us (16%)
  blocking collectives  55.3 us (15%)
  starting transfers between devices  32.6 us (9%)
  matrix products  25 us (7%)
  between operations  14.7 us (4%)
    all_gather x2, waiting for transfers between devices, entering(): pieces = jax.tree.map(lambda part: lax.all_gather(part, axis), subtotal)  79.9 us
    all_to_all x3, waiting for transfers between devices, several_exchanges(): lax.all_to_all(share, axis, split_axis=0, concat_axis=0, tiled=True)  38.7 us
    all_to_all x1, blocking collectives, several_exchanges(): lax.all_to_all(share, axis, split_axis=0, concat_axis=0, tiled=True)  31.1 us
    all_gather x2, blocking collectives, entering(): pieces = jax.tree.map(lambda part: lax.all_gather(part, axis), subtotal)  24.1 us
    convert_element_type x1, other arithmetic, conv_silu(): return jax.nn.silu(total).astype(jnp.bfloat16)  18.3 us
    unnamed x67, local copies, waits for them, and re-layouts  17 us
    all_to_all x3, starting transfers between devices, several_exchanges(): lax.all_to_all(share, axis, split_axis=0, concat_axis=0, tiled=True)  15.5 us
    mul x2, local copies, waits for them, and re-layouts, body(): values * norm_scale[..., None]  15.3 us
  transfers between devices with their start and end apart: 8, of which 4 were waited for; matrix products, arithmetic and copies ran while one was open for 13% of the time, Pallas kernels for 0%

commit v1 on v0

v1 whole, which is shorter than its diff:
```python
import functools
import math

import jax
import jax.numpy as jnp
from jax import lax
from jax.experimental import pallas as pl
from jax.experimental.pallas import tpu as pltpu
from jax.sharding import PartitionSpec as P

HEADS = 64
HEAD_DIM = 64
STATE = 128
GROUPS = 4
PER_GROUP = HEADS // GROUPS
GROUP_CH = PER_GROUP * HEAD_DIM
BLOCK = 256
D_IN = 4096
CH = 5120
L_DEV = 512
SHARDS = 16
OWN_CH = 256
SENT_ROWS = 136
PIECES = 2
PIECE_ROWS = 72
VMEM_LIMIT = 67043328
NORM_EPS = 1.0
LOG2E = math.log2(math.e)
CAP = 64.0

F32 = jnp.float32
BF16 = jnp.bfloat16


def dot(a, b):
    return lax.dot_general(a, b, (((1,), (0,)), ((), ())), preferred_element_type=F32)


def three_pieces(v):
    hi = v.astype(BF16).astype(F32)
    rest = v - hi
    mid = rest.astype(BF16).astype(F32)
    return hi, mid, (rest - mid).astype(BF16).astype(F32)


TAIL, GROWN = 0, 48


def spread_matrix(first):
    row = lax.broadcasted_iota(jnp.int32, (128, GROUP_CH), 0)
    col = lax.broadcasted_iota(jnp.int32, (128, GROUP_CH), 1)
    hit = (row >= first) & (row < first + 48) & (row % PER_GROUP == col // HEAD_DIM)
    return jnp.where(hit, 1.0, 0.0).astype(BF16)


def prep_kernel(step_ref, rate_ref, row_ref, sum_ref, col_ref):
    dt = jax.nn.softplus(step_ref[0])
    near = lax.broadcasted_iota(jnp.int32, (HEADS, HEADS), 0)
    far = lax.broadcasted_iota(jnp.int32, (HEADS, HEADS), 1)
    decay = jnp.sum(jnp.where(near == far, rate_ref[...], 0.0), axis=1, keepdims=True)
    rate = dt * (decay * -LOG2E)
    later = lax.broadcasted_iota(jnp.int32, (BLOCK, BLOCK), 0)
    earlier = lax.broadcasted_iota(jnp.int32, (BLOCK, BLOCK), 1)
    upto = jnp.where(later <= earlier, 1.0, 0.0).astype(BF16)
    zero = jnp.zeros((2 * PER_GROUP, BLOCK), F32)
    for j in range(L_DEV // BLOCK):
        span = slice(j * BLOCK, (j + 1) * BLOCK)
        dt_j = dt[:, span]
        stacked = jnp.concatenate(three_pieces(rate[:, span]), axis=0).astype(BF16)
        sums = dot(stacked, upto)
        cs = sums[:HEADS] + sums[HEADS : 2 * HEADS] + sums[2 * HEADS :]
        row_ref[:, span] = cs - jnp.log2(dt_j)
        tail = three_pieces(jnp.exp2(cs[:, BLOCK - 1 :] - cs) * dt_j)
        grown = three_pieces(jnp.exp2(cs))
        turned = jnp.transpose(jnp.concatenate([cs, cs], axis=0))
        for g in range(GROUPS):
            heads = slice(g * PER_GROUP, (g + 1) * PER_GROUP)
            parts = [v[heads] for v in tail + grown] + [zero]
            col_ref[g, span, :] = jnp.transpose(jnp.concatenate(parts, axis=0)).astype(BF16)
            sum_ref[g, span, :] = turned if g == 0 else pltpu.roll(turned, 128 - g * PER_GROUP, 1)


def prep(step_raw, decay_rate):
    return pl.pallas_call(
        prep_kernel,
        out_shape=(
            jax.ShapeDtypeStruct((HEADS, L_DEV), F32),
            jax.ShapeDtypeStruct((GROUPS, L_DEV, 128), F32),
            jax.ShapeDtypeStruct((GROUPS, L_DEV, 128), BF16),
        ),
        cost_estimate=pl.CostEstimate(flops=10**9, bytes_accessed=2**21, transcendentals=0),
        compiler_params=pltpu.CompilerParams(vmem_limit_bytes=VMEM_LIMIT),
        name="prep",
    )(step_raw, decay_rate)


CONV_ROWS = 32
CONV_AT = (0, 256, 640, 896)


def conv_kernel(
    prompt_ref, x_ref, b_ref, c_ref, hx_ref, hb_ref, hc_ref, wx_ref, wb_ref, wc_ref, bx_ref, bb_ref,
    bc_ref, last_ref, col_ref, xo_ref, bo_ref, co_ref, e0_ref, p_ref, xf, xs, spread, regrown,
):
    within = prompt_ref[0] % 4

    @pl.when(pl.program_id(0) == 0)
    def _():
        spread[...] = spread_matrix(TAIL)
        regrown[...] = spread_matrix(GROWN)


    def load(slot, ref, halo_ref, lanes):
        xf[slot, 5:8, :] = halo_ref[0, :, lanes].astype(F32)
        xf[slot, 8 : 8 + L_DEV, :] = ref[0, :, lanes].astype(F32)

    for k in range(8):
        load(k, x_ref, hx_ref, slice(k * 128, (k + 1) * 128))
    load(8, b_ref, hb_ref, slice(0, 128))
    load(9, c_ref, hc_ref, slice(0, 128))

    def taps(w_ref, bias_ref, lanes):
        w = w_ref[:, lanes].astype(F32) * 0.5
        return [w[k : k + 1] for k in range(4)], bias_ref[:, lanes].astype(F32) * 0.5

    def conved(slot, r0, w, bias):
        half = bias + w[0] * xf[slot, 5 + r0 : 5 + r0 + CONV_ROWS, :]
        for k in range(1, 4):
            half = half + w[k] * xf[slot, 5 + k + r0 : 5 + k + r0 + CONV_ROWS, :]
        return (half + half * jnp.tanh(half)).astype(BF16)

    for slot, w_ref, bias_ref, out in ((8, wb_ref, bb_ref, bo_ref), (9, wc_ref, bc_ref, co_ref)):
        w, bias = taps(w_ref, bias_ref, slice(0, 128))
        for r0 in range(0, L_DEV, CONV_ROWS):
            out[r0 : r0 + CONV_ROWS, :] = conved(slot, r0, w, bias)

    for pair in range(4):
        both = [taps(wx_ref, bx_ref, slice(k * 128, (k + 1) * 128)) for k in (2 * pair, 2 * pair + 1)]
        lanes2 = slice(pair * 256, (pair + 1) * 256)
        for r0 in range(0, L_DEV, CONV_ROWS):
            rows = slice(r0, r0 + CONV_ROWS)
            tail = dot(col_ref[0, rows, :], spread[:, lanes2])
            for half in range(2):
                k = 2 * pair + half
                lanes = slice(k * 128, (k + 1) * 128)
                value = conved(k, r0, *both[half])
                xo_ref[rows, lanes] = value
                xs[rows, lanes] = (value.astype(F32) * tail[:, half * 128 : half * 128 + 128]).astype(BF16)

    ends = jnp.concatenate([col_ref[0, 240:256, :], col_ref[0, 496:512, :]], axis=0)
    decays = dot(ends, regrown[...])
    first, second = decays[15:16], decays[31:32]
    last = last_ref[0].astype(F32)[12:16]
    bt = [
        jnp.transpose(bo_ref[j * BLOCK : (j + 1) * BLOCK, :].astype(F32)).astype(BF16) for j in range(2)
    ]
    for s in range(4):
        lanes = slice(s * OWN_CH, (s + 1) * OWN_CH)
        slot = s ^ within
        e0 = dot(bt[0], xs[:BLOCK, lanes])
        e1 = dot(bt[1], xs[BLOCK:, lanes])
        e0_ref[0, :, lanes] = e0.astype(BF16)
        p_ref[slot, :STATE, :] = (second[:, lanes] * e0 + e1).astype(BF16)
        hi, mid, _ = three_pieces(first[:, lanes] * second[:, lanes])
        at = CONV_AT[s]
        ends = [last[k : k + 1, at + 256 : at + 384] for k in range(4)]
        extra = [
            hi, mid, last[:, at : at + 256],
            jnp.concatenate(ends[:2], axis=1), jnp.concatenate(ends[2:], axis=1),
        ]
        p_ref[slot, STATE:, :] = jnp.concatenate(extra, axis=0).astype(BF16)


def conv(rows, before, weight, bias, cols, prompt):
    def at(height, width, first):
        return pl.BlockSpec((1, height, width), lambda g, p: (0, 0, first + g))

    def flat(height, width, first):
        return pl.BlockSpec((height, width), lambda g, p: (0, first + g))

    return pl.pallas_call(
        conv_kernel,
        grid_spec=pltpu.PrefetchScalarGridSpec(
            num_scalar_prefetch=1,
            grid=(GROUPS,),
            in_specs=[
                at(L_DEV, GROUP_CH, 0), at(L_DEV, 128, 32), at(L_DEV, 128, 36),
                at(3, GROUP_CH, 0), at(3, 128, 32), at(3, 128, 36),
                flat(4, GROUP_CH, 0), flat(4, 128, 32), flat(4, 128, 36),
                flat(1, GROUP_CH, 0), flat(1, 128, 32), flat(1, 128, 36),
                pl.BlockSpec((1, 16, CH // GROUPS), lambda g, p: (0, L_DEV // 16 - 1, g)),
                pl.BlockSpec((1, L_DEV, 128), lambda g, p: (g, 0, 0)),
            ],
            out_specs=(
                flat(L_DEV, GROUP_CH, 0),
                flat(L_DEV, 128, 0),
                flat(L_DEV, 128, 0),
                pl.BlockSpec((1, STATE, GROUP_CH), lambda g, p: (g, 0, 0)),
                pl.BlockSpec((4, SENT_ROWS, OWN_CH), lambda g, p: (g ^ (p[0] // 4), 0, 0)),
            ),
            scratch_shapes=[
                pltpu.VMEM((10, L_DEV + 8, 128), F32),
                pltpu.VMEM((L_DEV, GROUP_CH), BF16),
                pltpu.VMEM((128, GROUP_CH), BF16),
                pltpu.VMEM((128, GROUP_CH), BF16),
            ],
        ),
        out_shape=(
            jax.ShapeDtypeStruct((L_DEV, D_IN), BF16),
            jax.ShapeDtypeStruct((L_DEV, GROUPS * STATE), BF16),
            jax.ShapeDtypeStruct((L_DEV, GROUPS * STATE), BF16),
            jax.ShapeDtypeStruct((GROUPS, STATE, GROUP_CH), BF16),
            jax.ShapeDtypeStruct((SHARDS, SENT_ROWS, OWN_CH), BF16),
        ),
        cost_estimate=pl.CostEstimate(flops=10 * 10**9, bytes_accessed=14 * 2**20, transcendentals=0),
        compiler_params=pltpu.CompilerParams(vmem_limit_bytes=VMEM_LIMIT),
        name="conv_state",
    )(prompt, rows, rows, rows, before, before, before, weight, weight, weight, bias, bias, bias, rows, cols)


def intra_kernel(x_ref, b_ref, c_ref, row_ref, col_ref, y_ref):
    half = BLOCK // 2
    scores = lax.dot_general(
        c_ref[...], b_ref[...], (((1,), (1,)), ((), ())), preferred_element_type=F32
    )
    t = lax.broadcasted_iota(jnp.int32, (half, half), 0)
    u = lax.broadcasted_iota(jnp.int32, (half, half), 1)
    s00 = jnp.where(u <= t, scores[:half, :half], 0.0)
    s10 = scores[half:, :half]
    s11 = jnp.where(u <= t, scores[half:, half:], 0.0)
    low = lax.broadcasted_iota(jnp.int32, (BLOCK, 128), 1) < HEAD_DIM
    for pair in range(PER_GROUP // 2):
        lanes = slice(pair * 128, (pair + 1) * 128)
        x = x_ref[:, lanes]
        zero = jnp.zeros_like(x)
        xl, xh = jnp.where(low, x, zero), jnp.where(low, zero, x)
        top, bottom = [], []
        for h in (2 * pair, 2 * pair + 1):
            cs0 = jnp.broadcast_to(col_ref[0, :half, h : h + 1], (half, half))
            cs1 = jnp.broadcast_to(col_ref[0, half:, h : h + 1], (half, half))
            a0 = row_ref[h : h + 1, :half]
            a1 = row_ref[h : h + 1, half:]
            top.append((jnp.exp2(jnp.minimum(cs0 - a0, CAP)) * s00).astype(BF16))
            bottom.append((jnp.exp2(cs1 - a0) * s10).astype(BF16))
            bottom.append((jnp.exp2(jnp.minimum(cs1 - a1, CAP)) * s11).astype(BF16))
        above = dot(jnp.concatenate(top, axis=1), jnp.concatenate([xl[:half], xh[:half]], axis=0))
        below = dot(jnp.concatenate(bottom, axis=1), jnp.concatenate([xl, xh], axis=0))
        y_ref[:half, lanes] = above.astype(BF16)
        y_ref[half:, lanes] = below.astype(BF16)


def intra(x, b, c, sums, cols, groups, first):
    return pl.pallas_call(
        intra_kernel,
        grid=(groups, L_DEV // BLOCK),
        in_specs=[
            pl.BlockSpec((BLOCK, GROUP_CH), lambda g, j: (j, first + g)),
            pl.BlockSpec((BLOCK, 128), lambda g, j: (j, first + g)),
            pl.BlockSpec((BLOCK, 128), lambda g, j: (j, first + g)),
            pl.BlockSpec((PER_GROUP, BLOCK), lambda g, j: (first + g, j)),
            pl.BlockSpec((1, BLOCK, 128), lambda g, j: (first + g, j, 0)),
        ],
        out_specs=pl.BlockSpec((BLOCK, GROUP_CH), lambda g, j: (j, g)),
        out_shape=jax.ShapeDtypeStruct((L_DEV, groups * GROUP_CH), BF16),
        cost_estimate=pl.CostEstimate(
            flops=groups * 3 * 10**9, bytes_accessed=groups * 3 * 2**20, transcendentals=0
        ),
        compiler_params=pltpu.CompilerParams(vmem_limit_bytes=VMEM_LIMIT),
        name="intra",
    )(x, b, c, sums, cols)


def scan_kernel(r_ref, p_ref, *piece_refs):
    state = jnp.zeros((STATE, OWN_CH), F32)
    for d in range(SHARDS):
        p_ref[d] = state.astype(BF16)
        extra = r_ref[d, STATE:, :].astype(F32)
        state = (extra[0:1] + extra[1:2]) * state + r_ref[d, :STATE, :].astype(F32)
    size = STATE // PIECES
    zero = jnp.zeros((PIECE_ROWS - size - 3, OWN_CH), F32)
    for k, ref in enumerate(piece_refs):
        rows = extra[2 + 2 * k : 4 + 2 * k]
        parts = [state[k * size : k * size + size], rows, extra[6 + k : 7 + k], zero]
        ref[...] = jnp.concatenate(parts, axis=0).astype(BF16)


def scan(got):
    piece = jax.ShapeDtypeStruct((PIECE_ROWS, OWN_CH), BF16)
    out = pl.pallas_call(
        scan_kernel,
        out_shape=[jax.ShapeDtypeStruct((SHARDS, STATE, OWN_CH), BF16)] + [piece] * PIECES,
        cost_estimate=pl.CostEstimate(flops=10**9, bytes_accessed=2**22, transcendentals=0),
        compiler_params=pltpu.CompilerParams(vmem_limit_bytes=VMEM_LIMIT),
        name="scan",
    )(got)
    return out[0], out[1:]


def pack_kernel(place_ref, prompt_ref, owner_ref, *refs):
    pieces, p_ref = refs[:-1], refs[-1]
    p_ref[...] = jnp.zeros_like(p_ref)
    for k in range(PIECES):
        p_ref[owner_ref[place_ref[0] ^ prompt_ref[0] ^ k]] = pieces[k][...]


SMEM = pl.BlockSpec(memory_space=pltpu.SMEM)
VMEM = pl.BlockSpec(memory_space=pltpu.VMEM)


def pack(place, prompt, owner_slot, pieces):
    return pl.pallas_call(
        pack_kernel,
        in_specs=[SMEM] * 3 + [VMEM] * PIECES,
        out_shape=jax.ShapeDtypeStruct((SHARDS, PIECE_ROWS, OWN_CH), BF16),
        cost_estimate=pl.CostEstimate(flops=10**8, bytes_accessed=2**19, transcendentals=0),
        compiler_params=pltpu.CompilerParams(vmem_limit_bytes=VMEM_LIMIT),
        name="pack",
    )(place, prompt, owner_slot, *pieces)


def unpack_kernel(place_ref, prompt_ref, owner_ref, r_ref, ssm_ref, conv_ref):
    size = STATE // PIECES
    mine = 0
    for p in range(SHARDS):
        mine = jnp.where(owner_ref[p] == place_ref[0], p, mine)
    parts = [r_ref[mine ^ prompt_ref[0] ^ k].astype(F32) for k in range(PIECES)]
    state = jnp.concatenate([part[:size] for part in parts], axis=0)
    ssm_ref[...] = jnp.transpose(state)
    rows = jnp.concatenate([part[size : size + 2] for part in parts], axis=0)
    ends = [part[size + 2 : size + 3, n * 128 : n * 128 + 128] for part in parts for n in range(2)]
    window = jnp.concatenate([rows, jnp.concatenate(ends, axis=0)], axis=1)
    moved = jnp.concatenate([window[:, 64:], window[:, :64]], axis=1)
    odd = prompt_ref[0] % 2 == 1
    conv_ref[...] = jnp.where(odd, moved, window)[:, : CH // SHARDS].astype(BF16)


def unpack(place, prompt, owner_slot, got):
    return pl.pallas_call(
        unpack_kernel,
        in_specs=[SMEM] * 3 + [VMEM],
        out_shape=(
            jax.ShapeDtypeStruct((OWN_CH, STATE), F32),
            jax.ShapeDtypeStruct((4, CH // SHARDS), BF16),
        ),
        cost_estimate=pl.CostEstimate(flops=10**8, bytes_accessed=2**19, transcendentals=0),
        compiler_params=pltpu.CompilerParams(vmem_limit_bytes=VMEM_LIMIT),
        name="unpack",
    )(place, prompt, owner_slot, got)


def out_kernel(prompt_ref, y_ref, c_ref, col_ref, e0_ref, state_ref, gain_ref, o_ref, ys, spread):
    within = prompt_ref[0] % 4

    @pl.when(pl.program_id(0) == 0)
    def _():
        spread[...] = spread_matrix(GROWN)

    decay = dot(col_ref[0, 240:256, :], spread[...])[15:16]
    for j in range(2):
        rows = slice(j * BLOCK, (j + 1) * BLOCK)
        c = c_ref[rows, :]
        grown = col_ref[0, rows, :]
        total = jnp.zeros((BLOCK, 128), F32)
        for s in range(4):
            lanes = slice(s * OWN_CH, (s + 1) * OWN_CH)
            state = state_ref[s ^ within]
            if j == 1:
                state = (decay[:, lanes] * state.astype(F32) + e0_ref[0, :, lanes].astype(F32)).astype(BF16)
            y = y_ref[rows, lanes].astype(F32) + dot(grown, spread[:, lanes]) * dot(c, state)
            ys[:, lanes] = y
            total = total + y[:, :128] * y[:, :128] + y[:, 128:] * y[:, 128:]
        mean = jnp.sum(total, axis=1, keepdims=True) * (1.0 / GROUP_CH)
        scale = lax.rsqrt(mean + NORM_EPS)
        o_ref[0, rows, :] = (ys[...] * scale * gain_ref[...]).astype(BF16)


def finish(y, c, cols, e0, states, gain, prompt):
    return pl.pallas_call(
        out_kernel,
        grid_spec=pltpu.PrefetchScalarGridSpec(
            num_scalar_prefetch=1,
            grid=(GROUPS,),
            in_specs=[
                pl.BlockSpec((L_DEV, GROUP_CH), lambda g, p: (0, g)),
                pl.BlockSpec((L_DEV, 128), lambda g, p: (0, g)),
                pl.BlockSpec((1, L_DEV, 128), lambda g, p: (g, 0, 0)),
                pl.BlockSpec((1, STATE, GROUP_CH), lambda g, p: (g, 0, 0)),
                pl.BlockSpec((4, STATE, OWN_CH), lambda g, p: (g ^ (p[0] // 4), 0, 0)),
                pl.BlockSpec((1, GROUP_CH), lambda g, p: (0, g)),
            ],
            out_specs=pl.BlockSpec((1, L_DEV, GROUP_CH), lambda g, p: (0, 0, g)),
            scratch_shapes=[pltpu.VMEM((BLOCK, GROUP_CH), F32), pltpu.VMEM((128, GROUP_CH), BF16)],
        ),
        out_shape=jax.ShapeDtypeStruct((1, L_DEV, D_IN), BF16),
        cost_estimate=pl.CostEstimate(flops=8 * 10**9, bytes_accessed=12 * 2**20, transcendentals=0),
        compiler_params=pltpu.CompilerParams(vmem_limit_bytes=VMEM_LIMIT),
        name="finish",
    )(prompt, y, c, cols, e0, states, gain)


def exchange(pieces, axis):
    return lax.all_to_all(pieces, axis, split_axis=0, concat_axis=0, tiled=True)


def body(conv_input, step_raw, decay_rate, conv_weight, conv_bias, norm_gain, owner_slot):
    place = lax.axis_index("seq").astype(jnp.int32)[None]
    prompt = lax.axis_index("grp").astype(jnp.int32)[None]
    route = [(d, d + 1) for d in range(SHARDS - 1)]
    before = lax.ppermute(conv_input[:, L_DEV - 3 :, :], "seq", route)
    starts, sums, cols = prep(step_raw, decay_rate[None, :])
    x, b, c, e0, sent = conv(conv_input, before, conv_weight, conv_bias[None, :], cols, prompt)
    y = intra(x, b, c, starts, sums, GROUPS, 0)
    got, y = lax.optimization_barrier((exchange(sent, "seq"), y))
    states, final = scan(got)
    entering = exchange(states, "seq")
    pieces = []
    for k in range(PIECES):
        route = [
            (r * SHARDS + p, (r ^ k) * SHARDS + (r ^ p)) for r in range(SHARDS) for p in range(SHARDS)
        ]
        pieces.append(lax.ppermute(final[k], ("seq", "grp"), route))
    packed = pack(place, prompt, owner_slot, pieces)
    entering, packed = lax.optimization_barrier((entering, packed))
    arrived = exchange(packed, "seq")
    mixed = finish(y, c, cols, e0, entering, norm_gain[None, :], prompt)
    ssm, rows = unpack(place, prompt, owner_slot, arrived)
    return mixed, ssm.reshape(1, 4, HEAD_DIM, STATE), jnp.transpose(rows)[None]


def solution(mesh):
    return jax.shard_map(
        body,
        mesh=mesh,
        in_specs=(P("grp", "seq", None), P("grp", None, "seq"), P(), P(), P(), P(), P()),
        out_specs=(P("grp", "seq", None), P("seq", "grp", None, None), P("seq", "grp", None)),
        check_vma=False,
    )
```

time: 370 us -> 92.8 us (0.25)
  waiting for transfers between devices: 119 us -> 18 us
  other arithmetic: 62.5 us -> 0 us
  local copies, waits for them, and re-layouts: 58.7 us -> 2.84 us
  blocking collectives: 55.3 us -> 0 us
  Pallas kernels: 0 us -> 38.9 us
  matrix products: 25 us -> 0 us
  between operations: 14.7 us -> 0.67 us
    all_gather x2 -> x0, waiting for transfers between devices: 79.9 us -> none  [entering(): pieces = jax.tree.map(lambda part: lax.all_gather(part, axis), subtotal)]
    pallas_call x0 -> x7, Pallas kernels: none -> 38.9 us  [the longest x1 11.6 us: conv(): pl.pallas_call(conv_kernel, grid_spec=pltpu.PrefetchScalarGridSpec(num_sc...]
    all_to_all x1 -> x0, blocking collectives: 31.1 us -> none  [several_exchanges(): lax.all_to_all(share, axis, split_axis=0, concat_axis=0, tiled=True)]
    all_to_all x5 -> x3, waiting for transfers between devices: 38.7 us -> 9.37 us  [exchange(): return lax.all_to_all(pieces, axis, split_axis=0, concat_axis=0, tiled=True)]
    convert_element_type x7 -> x0, other arithmetic: 28.4 us -> none  [the longest x1 18.3 us: conv_silu(): return jax.nn.silu(total).astype(jnp.bfloat16)]
    dot_general x8 -> x0, matrix products: 25 us -> none  [the longest x2 10.3 us: block_terms(): jnp.einsum('gkun,ugkp->gkpn', scaled, inputs, preferred_element_type=jnp....]
    all_gather x2 -> x0, blocking collectives: 24.1 us -> none  [entering(): pieces = jax.tree.map(lambda part: lax.all_gather(part, axis), subtotal)]
    unnamed x67 -> x0, local copies, waits for them, and re-layouts: 17 us -> none
  transfers between devices with their start and end apart: 8 -> 6, of which waited for: 4 -> 3; matrix products, arithmetic and copies ran while one was open for 13% -> 1% of each run, Pallas kernels for 0% -> 25%
where the time goes in v1:
time: 92.8 us; the launch traced here: 91.8 us
  Pallas kernels  38.9 us (42%)
  starting transfers between devices  31.4 us (34%)
  waiting for transfers between devices  18 us (19%)
  local copies, waits for them, and re-layouts  2.84 us (3%)
    all_to_all x3, starting transfers between devices, exchange(): return lax.all_to_all(pieces, axis, split_axis=0, concat_axis=0, tiled=True)  20.5 us
    pallas_call x1, Pallas kernels, conv(): pl.pallas_call(conv_kernel, grid_spec=pltpu.PrefetchScalarGridSpec(num_sc...  11.6 us
    pallas_call x1, Pallas kernels, intra(): pl.pallas_call(intra_kernel, grid=(groups, L_DEV // BLOCK), in_specs=[pl....  10.8 us
    all_to_all x3, waiting for transfers between devices, exchange(): return lax.all_to_all(pieces, axis, split_axis=0, concat_axis=0, tiled=True)  9.37 us
    ppermute x2, waiting for transfers between devices, body(): pieces.append(lax.ppermute(final[k], ('seq', 'grp'), route))  8.65 us
    pallas_call x1, Pallas kernels, finish(): pl.pallas_call(out_kernel, grid_spec=pltpu.PrefetchScalarGridSpec(num_sca...  7.41 us
    ppermute x2, starting transfers between devices, body(): pieces.append(lax.ppermute(final[k], ('seq', 'grp'), route))  6.39 us
    ppermute x1, starting transfers between devices, body(): before = lax.ppermute(conv_input[:, L_DEV - 3:, :], 'seq', route)  4.54 us
  transfers between devices with their start and end apart: 6, of which 3 were waited for; matrix products, arithmetic and copies ran while one was open for 1% of the time, Pallas kernels for 25%

profile of v1, /device:TPU:1, one launch (start us, length us, event | category | flops | bytes accessed | tf_op | source)
XLA Modules:
  0.0 91.8 jit_solution(3320185051510515238)
XLA Ops:
  0.6 1.5 %slice.3 = bf16[1,3,5120]{2,1,0:T(4,128)(2,1)} slice(bf16[1,512,5120]{2,1,0:T(8,128)(2,1)} %last_ref.1), slice={[0:1], [509:512], [0:5120]} | slice | bytes 61440 | tf_op jit(solution)/shard_map/slice | solution.py:409
  2.2 4.5 %collective-permute-start = (bf16[1,3,5120]{2,1,0:T(4,128)(2,1)}, bf16[1,3,5120]{2,1,0:T(4,128)(2,1)}, u32[]{:S(2)}, u32[]{:S(2)}) collective-permute-start(bf16[1,3,5120]{2,1,0:T(4,128)(2,1)} %slice.3), channel_id=1, source_target_pairs={{0,16},{16,32},{32,48},{48,64},{64,80},{80,96},{96,112},{112,128},... | collective-permute-start | bytes 92168 | tf_op jit(solution)/shard_map/ppermute | solution.py:409
  6.7 3.1 %prep.1 = (f32[64,512]{1,0:T(8,128)}, f32[4,512,128]{2,1,0:T(8,128)}, bf16[4,512,128]{2,1,0:T(8,128)(2,1)}) custom-call(f32[1,64,512]{2,1,0:T(8,128)} %step_ref.1, f32[1,64]{1,0:T(1,128)} %bitcast.11), custom_call_target="tpu_custom_call" | custom-call | flops 1000000000 | bytes 2097152 | tf_op jit(solution)/shard_map/prep/pallas_call | solution.py:84
  9.8 1.3 %broadcast_in_dim.19.bx_ref.bb_ref.bc_ref = bf16[1,5120]{1,0:T(2,128)(2,1)} reshape(bf16[5120]{0:T(1024)(128)(2,1)} %param.11) | data formatting | bytes 20480 | tf_op jit(solution)/shard_map/broadcast_in_dim | solution.py:411
  11.1 0.0 collective-permute-done.hx_ref.hb_ref.hc_ref
  11.1 11.6 %conv_state.1 = (bf16[512,4096]{1,0:T(8,128)(2,1)}, bf16[512,512]{1,0:T(8,128)(2,1)}, bf16[512,512]{1,0:T(8,128)(2,1)}, bf16[4,128,1024]{2,1,0:T(8,128)(2,1)}, bf16[16,136,256]{2,1,0:T(8,128)(2,1)}) custom-call(s32[1]{0:T(128)} %bitcast.prompt_ref, bf16[1,512,5120]{2,1,0:T(8,128)(2,1)} %last_ref.1, bf16[1,512,5120]{2,1,0:T(8,128)(2,1)} %last_ref.1, ...), custom_call_target="tpu_custom_call" | custom-call | flops 10000000000 | bytes 14680064 | tf_op jit(solution)/shard_map/conv_state/pallas_call | solution.py:181
  22.7 5.9 %all-to-all-start = ((bf16[16,136,256]{2,1,0:T(8,128)(2,1)}), bf16[16,136,256]{2,1,0:T(8,128)(2,1)}, u32[]{:S(2)}, u32[]{:S(2)}) async-start(bf16[16,136,256]{2,1,0:T(8,128)(2,1)} %get-tuple-element.21), calls=%async_computation | async-start | bytes 2228224 | tf_op jit(solution)/shard_map/all_to_all | solution.py:402
  28.6 10.8 %intra.1.y_ref = bf16[512,4096]{1,0:T(8,128)(2,1)} custom-call(bf16[512,4096]{1,0:T(8,128)(2,1)} %get-tuple-element.22.x_ref, bf16[512,512]{1,0:T(8,128)(2,1)} %get-tuple-element.23.b_ref, bf16[512,512]{1,0:T(8,128)(2,1)} %get-tuple-element.24.c_ref, f32[64,512]{1,0:T(8,128)} %get-tuple-element.25.row_ref, f32[4,512,128]{2,1,0:T(8,128)} %get-tuple-element.26.col_ref), custom_call_target="tpu_custom_call" | custom-call | flops 12000000000 | bytes 12582912 | tf_op jit(solution)/shard_map/intra/pallas_call | solution.py:253
  39.4 5.7 %all-to-all-done.r_ref = bf16[16,136,256]{2,1,0:T(8,128)(2,1)} async-done(((bf16[16,136,256]{2,1,0:T(8,128)(2,1)}), bf16[16,136,256]{2,1,0:T(8,128)(2,1)}, u32[]{:S(2)}, u32[]{:S(2)}) %all-to-all-start) | async-done | bytes 1114144 | tf_op jit(solution)/shard_map/all_to_all | solution.py:402
  45.1 2.5 %scan.1 = (bf16[16,128,256]{2,1,0:T(8,128)(2,1)}, bf16[72,256]{1,0:T(8,128)(2,1)}, bf16[72,256]{1,0:T(8,128)(2,1)}) custom-call(bf16[16,136,256]{2,1,0:T(8,128)(2,1)} %all-to-all-done.r_ref), custom_call_target="tpu_custom_call" | custom-call | flops 1000000000 | bytes 4194304 | tf_op jit(solution)/shard_map/scan/pallas_call | solution.py:289
  47.6 4.4 %all-to-all-start.1 = ((bf16[16,128,256]{2,1,0:T(8,128)(2,1)}), bf16[16,128,256]{2,1,0:T(8,128)(2,1)}, u32[]{:S(2)}, u32[]{:S(2)}) async-start(bf16[16,128,256]{2,1,0:T(8,128)(2,1)} %get-tuple-element.30), calls=%async_computation.1 | async-start | bytes 2097152 | tf_op jit(solution)/shard_map/all_to_all | solution.py:402
  52.0 2.0 %collective-permute-start.1 = (bf16[72,256]{1,0:T(8,128)(2,1)}, bf16[72,256]{1,0:T(8,128)(2,1)}, u32[]{:S(2)}, u32[]{:S(2)}) collective-permute-start(bf16[72,256]{1,0:T(8,128)(2,1)} %get-tuple-element.31), channel_id=1, source_target_pairs={{0,0},{1,1},{2,2},{3,3},{4,4},{5,5},{6,6},{7,7},{8,8},{9,9},{10,10... | collective-permute-start | bytes 110600 | tf_op jit(solution)/shard_map/ppermute | solution.py:421
  54.0 4.4 %collective-permute-start.2 = (bf16[72,256]{1,0:T(8,128)(2,1)}, bf16[72,256]{1,0:T(8,128)(2,1)}, u32[]{:S(2)}, u32[]{:S(2)}) collective-permute-start(bf16[72,256]{1,0:T(8,128)(2,1)} %get-tuple-element.32), channel_id=1, source_target_pairs={{0,16},{1,17},{2,18},{3,19},{4,20},{5,21},{6,22},{7,23},{8,24},{9,... | collective-permute-start | bytes 110600 | tf_op jit(solution)/shard_map/ppermute | solution.py:421
  58.4 0.0 collective-permute-done.1.refs_0_
  58.4 8.6 %collective-permute-done.2.refs_1_ = bf16[72,256]{1,0:T(8,128)(2,1)} collective-permute-done((bf16[72,256]{1,0:T(8,128)(2,1)}, bf16[72,256]{1,0:T(8,128)(2,1)}, u32[]{:S(2)}, u32[]{:S(2)}) %collective-permute-start.2) | collective-permute-done | bytes 36896 | tf_op jit(solution)/shard_map/ppermute | solution.py:421
  67.0 1.7 %pack.1 = bf16[16,72,256]{2,1,0:T(8,128)(2,1)} custom-call(s32[1]{0:T(128)} %bitcast.2.place_ref, s32[1]{0:T(128)} %bitcast.prompt_ref, s32[16]{0:T(128)} %owner_ref.3, bf16[72,256]{1,0:T(8,128)(2,1)} %collective-permute-done.1.refs_0_, bf16[72,256]{1,0:T(8,128)(2,1)} %collective-permute-done.2.refs_1_), custom_call_target="tpu_custom_call" | custom-call | flops 100000000 | bytes 524288 | tf_op jit(solution)/shard_map/pack/pallas_call | solution.py:311
  68.7 0.0 all-to-all-done.1.state_ref
  68.7 10.2 %all-to-all-start.2 = ((bf16[16,72,256]{2,1,0:T(8,128)(2,1)}), bf16[16,72,256]{2,1,0:T(8,128)(2,1)}, u32[]{:S(2)}, u32[]{:S(2)}) async-start(bf16[16,72,256]{2,1,0:T(8,128)(2,1)} %pack.1), calls=%async_computation.2 | async-start | bytes 1179648 | tf_op jit(solution)/shard_map/all_to_all | solution.py:402
  78.9 7.4 %finish.1 = bf16[1,512,4096]{2,1,0:T(8,128)(2,1)} custom-call(s32[1]{0:T(128)} %bitcast.prompt_ref, bf16[512,4096]{1,0:T(8,128)(2,1)} %intra.1.y_ref, bf16[512,512]{1,0:T(8,128)(2,1)} %get-tuple-element.24.c_ref, bf16[4,512,128]{2,1,0:T(8,128)(2,1)} %get-tuple-element.20.col_ref, bf16[4,128,1024]{2,1,0:T(8,128)(2,1)} %get-tuple-element.28.e0_ref, ...), custom_call_target="tpu_custom_call" | custom-call | flops 8000000000 | bytes 12582912 | tf_op jit(solution)/shard_map/finish/pallas_call | solution.py:378
  86.4 3.6 %all-to-all-done.2.r_ref = bf16[16,72,256]{2,1,0:T(8,128)(2,1)} async-done(((bf16[16,72,256]{2,1,0:T(8,128)(2,1)}), bf16[16,72,256]{2,1,0:T(8,128)(2,1)}, u32[]{:S(2)}, u32[]{:S(2)}) %all-to-all-start.2) | async-done | bytes 589856 | tf_op jit(solution)/shard_map/all_to_all | solution.py:402
  90.0 1.8 %unpack.1 = (f32[256,128]{1,0:T(8,128)}, bf16[4,320]{1,0:T(4,128)(2,1)}) custom-call(s32[1]{0:T(128)} %bitcast.2.place_ref, s32[1]{0:T(128)} %bitcast.prompt_ref, s32[16]{0:T(128)} %owner_ref.3, bf16[16,72,256]{2,1,0:T(8,128)(2,1)} %all-to-all-done.2.r_ref), custom_call_target="tpu_custom_call" | custom-call | flops 100000000 | bytes 524288 | tf_op jit(solution)/shard_map/unpack/pallas_call | solution.py:338
Async XLA Ops:
  2.2 9.0 %collective-permute-start = (bf16[1,3,5120]{2,1,0:T(4,128)(2,1)}, bf16[1,3,5120]{2,1,0:T(4,128)(2,1)}, u32[]{:S(2)}, u32[]{:S(2)}) collective-permute-start(bf16[1,3,5120]{2,1,0:T(4,128)(2,1)} %slice.3), channel_id=1, source_target_pairs={{0,16},{16,32},{32,48},{48,64},{64,80},{80,96},{96,112},{112,128},... | collective-permute-start | bytes 92168 | tf_op jit(solution)/shard_map/ppermute | solution.py:409
  22.7 22.4 %all-to-all-start = ((bf16[16,136,256]{2,1,0:T(8,128)(2,1)}), bf16[16,136,256]{2,1,0:T(8,128)(2,1)}, u32[]{:S(2)}, u32[]{:S(2)}) async-start(bf16[16,136,256]{2,1,0:T(8,128)(2,1)} %get-tuple-element.21), calls=%async_computation | async-start | bytes 2228224 | tf_op jit(solution)/shard_map/all_to_all | solution.py:402
  47.6 21.1 %all-to-all-start.1 = ((bf16[16,128,256]{2,1,0:T(8,128)(2,1)}), bf16[16,128,256]{2,1,0:T(8,128)(2,1)}, u32[]{:S(2)}, u32[]{:S(2)}) async-start(bf16[16,128,256]{2,1,0:T(8,128)(2,1)} %get-tuple-element.30), calls=%async_computation.1 | async-start | bytes 2097152 | tf_op jit(solution)/shard_map/all_to_all | solution.py:402
  52.0 6.4 %collective-permute-start.1 = (bf16[72,256]{1,0:T(8,128)(2,1)}, bf16[72,256]{1,0:T(8,128)(2,1)}, u32[]{:S(2)}, u32[]{:S(2)}) collective-permute-start(bf16[72,256]{1,0:T(8,128)(2,1)} %get-tuple-element.31), channel_id=1, source_target_pairs={{0,0},{1,1},{2,2},{3,3},{4,4},{5,5},{6,6},{7,7},{8,8},{9,9},{10,10... | collective-permute-start | bytes 110600 | tf_op jit(solution)/shard_map/ppermute | solution.py:421
  54.0 13.0 %collective-permute-start.2 = (bf16[72,256]{1,0:T(8,128)(2,1)}, bf16[72,256]{1,0:T(8,128)(2,1)}, u32[]{:S(2)}, u32[]{:S(2)}) collective-permute-start(bf16[72,256]{1,0:T(8,128)(2,1)} %get-tuple-element.32), channel_id=1, source_target_pairs={{0,16},{1,17},{2,18},{3,19},{4,20},{5,21},{6,22},{7,23},{8,24},{9,... | collective-permute-start | bytes 110600 | tf_op jit(solution)/shard_map/ppermute | solution.py:421
  68.7 21.3 %all-to-all-start.2 = ((bf16[16,72,256]{2,1,0:T(8,128)(2,1)}), bf16[16,72,256]{2,1,0:T(8,128)(2,1)}, u32[]{:S(2)}, u32[]{:S(2)}) async-start(bf16[16,72,256]{2,1,0:T(8,128)(2,1)} %pack.1), calls=%async_computation.2 | async-start | bytes 1179648 | tf_op jit(solution)/shard_map/all_to_all | solution.py:402

commit v2 on v1

v2 whole, which is shorter than its diff:
```python
import functools
import math

import jax
import jax.numpy as jnp
from jax import lax
from jax.experimental import pallas as pl
from jax.experimental.pallas import tpu as pltpu
from jax.sharding import PartitionSpec as P

HEADS = 64
HEAD_DIM = 64
STATE = 128
GROUPS = 4
PER_GROUP = HEADS // GROUPS
GROUP_CH = PER_GROUP * HEAD_DIM
BLOCK = 256
D_IN = 4096
CH = 5120
L_DEV = 512
SHARDS = 16
OWN_CH = 256
SENT_ROWS = 136
PIECES = 2
FLIP = SHARDS - 1
PIECE_ROWS = 72
VMEM_LIMIT = 67043328
NORM_EPS = 1.0
LOG2E = math.log2(math.e)
CAP = 64.0

SMEM = pl.BlockSpec(memory_space=pltpu.SMEM)
VMEM = pl.BlockSpec(memory_space=pltpu.VMEM)
ANY = pl.BlockSpec(memory_space=pl.ANY)

F32 = jnp.float32
BF16 = jnp.bfloat16


def dot(a, b):
    return lax.dot_general(a, b, (((1,), (0,)), ((), ())), preferred_element_type=F32)


def three_pieces(v):
    hi = v.astype(BF16).astype(F32)
    rest = v - hi
    mid = rest.astype(BF16).astype(F32)
    return hi, mid, (rest - mid).astype(BF16).astype(F32)


TAIL, GROWN = 0, 48


def spread_matrix(first):
    row = lax.broadcasted_iota(jnp.int32, (128, GROUP_CH), 0)
    col = lax.broadcasted_iota(jnp.int32, (128, GROUP_CH), 1)
    hit = (row >= first) & (row < first + 48) & (row % PER_GROUP == col // HEAD_DIM)
    return jnp.where(hit, 1.0, 0.0).astype(BF16)


def prep_kernel(step_ref, rate_ref, row_ref, sum_ref, col_ref):
    dt = jax.nn.softplus(step_ref[0])
    near = lax.broadcasted_iota(jnp.int32, (HEADS, HEADS), 0)
    far = lax.broadcasted_iota(jnp.int32, (HEADS, HEADS), 1)
    decay = jnp.sum(jnp.where(near == far, rate_ref[...], 0.0), axis=1, keepdims=True)
    rate = dt * (decay * -LOG2E)
    later = lax.broadcasted_iota(jnp.int32, (BLOCK, BLOCK), 0)
    earlier = lax.broadcasted_iota(jnp.int32, (BLOCK, BLOCK), 1)
    upto = jnp.where(later <= earlier, 1.0, 0.0).astype(BF16)
    zero = jnp.zeros((2 * PER_GROUP, BLOCK), F32)
    for j in range(L_DEV // BLOCK):
        span = slice(j * BLOCK, (j + 1) * BLOCK)
        dt_j = dt[:, span]
        stacked = jnp.concatenate(three_pieces(rate[:, span]), axis=0).astype(BF16)
        sums = dot(stacked, upto)
        cs = sums[:HEADS] + sums[HEADS : 2 * HEADS] + sums[2 * HEADS :]
        row_ref[:, span] = cs - jnp.log2(dt_j)
        tail = three_pieces(jnp.exp2(cs[:, BLOCK - 1 :] - cs) * dt_j)
        grown = three_pieces(jnp.exp2(cs))
        sum_ref[span, :] = jnp.transpose(jnp.concatenate([cs, cs], axis=0))
        for g in range(GROUPS):
            heads = slice(g * PER_GROUP, (g + 1) * PER_GROUP)
            parts = [v[heads] for v in tail + grown] + [zero]
            col_ref[g, span, :] = jnp.transpose(jnp.concatenate(parts, axis=0)).astype(BF16)


def prep(step_raw, decay_rate):
    return pl.pallas_call(
        prep_kernel,
        out_shape=(
            jax.ShapeDtypeStruct((HEADS, L_DEV), F32),
            jax.ShapeDtypeStruct((L_DEV, 2 * HEADS), F32),
            jax.ShapeDtypeStruct((GROUPS, L_DEV, 128), BF16),
        ),
        cost_estimate=pl.CostEstimate(flops=10**9, bytes_accessed=2**21, transcendentals=0),
        compiler_params=pltpu.CompilerParams(vmem_limit_bytes=VMEM_LIMIT),
        name="prep",
    )(step_raw, decay_rate)


CONV_ROWS = 16


def taps(w_ref, bias_ref, lanes):
    w = w_ref[:, lanes].astype(F32) * 0.5
    return [w[k : k + 1] for k in range(4)], bias_ref[:, lanes].astype(F32) * 0.5


def silu_of(values, at, w, bias):
    half = bias + w[0] * values[at : at + CONV_ROWS, :]
    for k in range(1, 4):
        half = half + w[k] * values[at + k : at + k + CONV_ROWS, :]
    return half + half * jnp.tanh(half)


def conv_kernel(
    mask_ref, x_ref, b_ref, hx_ref, hb_ref, wx_ref, wb_ref, bx_ref, bb_ref, last_ref, col_ref,
    xo_ref, bo_ref, e0_ref, p_ref, xf, xs, tails, spread, regrown,
):
    within = mask_ref[0] % 4

    @pl.when(pl.program_id(0) == 0)
    def _():
        spread[...] = spread_matrix(TAIL)
        regrown[...] = spread_matrix(GROWN)

    def load(slot, ref, halo_ref, lanes):
        xf[slot, 5:8, :] = halo_ref[0, :, lanes].astype(F32)
        xf[slot, 8 : 8 + L_DEV, :] = ref[0, :, lanes].astype(F32)

    load(8, b_ref, hb_ref, slice(0, 128))
    w, bias = taps(wb_ref, bb_ref, slice(0, 128))
    for r0 in range(0, L_DEV, CONV_ROWS):
        bo_ref[r0 : r0 + CONV_ROWS, :] = silu_of(xf.at[8], 5 + r0, w, bias).astype(BF16)
    bt = [
        jnp.transpose(bo_ref[j * BLOCK : (j + 1) * BLOCK, :].astype(F32)).astype(BF16) for j in range(2)
    ]
    ends = jnp.concatenate([col_ref[0, 240:256, :], col_ref[0, 496:512, :]], axis=0)
    decays = dot(ends, regrown[...])
    last = last_ref[0].astype(F32)[12:16]
    for s in range(4):
        wide = slice(s * OWN_CH, (s + 1) * OWN_CH)
        tails[s] = dot(col_ref[0], spread[:, wide])
        pair = (2 * s, 2 * s + 1)
        both = []
        for k in pair:
            lanes = slice(k * 128, (k + 1) * 128)
            load(k, x_ref, hx_ref, lanes)
            both.append(taps(wx_ref, bx_ref, lanes))
        for r0 in range(0, L_DEV, CONV_ROWS):
            rows = slice(r0, r0 + CONV_ROWS)
            parts = [silu_of(xf.at[k], 5 + r0, *tap) for k, tap in zip(pair, both)]
            value = jnp.concatenate(parts, axis=1)
            xo_ref[rows, wide] = value.astype(BF16)
            xs[rows, wide] = (value * tails[s, rows, :]).astype(BF16)
        first, second = decays[15:16, wide], decays[31:32, wide]
        e0 = dot(bt[0], xs[:BLOCK, wide])
        e1 = dot(bt[1], xs[BLOCK:, wide])
        e0_ref[0, :, wide] = e0.astype(BF16)
        slot = s ^ within
        p_ref[slot, :STATE, :] = (second * e0 + e1).astype(BF16)
        hi, mid, _ = three_pieces(first * second)
        at = CONV_AT[s]
        ends_of = [last[k : k + 1, at + 256 : at + 384] for k in range(4)]
        extra = [
            hi, mid, last[:, at : at + 256],
            jnp.concatenate(ends_of[:2], axis=1), jnp.concatenate(ends_of[2:], axis=1),
        ]
        p_ref[slot, STATE:, :] = jnp.concatenate(extra, axis=0).astype(BF16)


CONV_AT = (0, 256, 640, 896)


def conv(rows, before, weight, bias, cols, mask):
    def whole(height, width, first):
        return pl.BlockSpec((1, height, width), lambda g, p: (0, 0, first + g))

    def flat(height, width, first):
        return pl.BlockSpec((height, width), lambda g, p: (0, first + g))

    return pl.pallas_call(
        conv_kernel,
        grid_spec=pltpu.PrefetchScalarGridSpec(
            num_scalar_prefetch=1,
            grid=(GROUPS,),
            in_specs=[
                whole(L_DEV, GROUP_CH, 0), whole(L_DEV, 128, 32),
                whole(3, GROUP_CH, 0), whole(3, 128, 32),
                flat(4, GROUP_CH, 0), flat(4, 128, 32),
                flat(1, GROUP_CH, 0), flat(1, 128, 32),
                pl.BlockSpec((1, 16, CH // GROUPS), lambda g, p: (0, L_DEV // 16 - 1, g)),
                pl.BlockSpec((1, L_DEV, 128), lambda g, p: (g, 0, 0)),
            ],
            out_specs=(
                flat(L_DEV, GROUP_CH, 0),
                flat(L_DEV, 128, 0),
                pl.BlockSpec((1, STATE, GROUP_CH), lambda g, p: (g, 0, 0)),
                pl.BlockSpec((4, SENT_ROWS, OWN_CH), lambda g, p: (g ^ (p[0] // 4), 0, 0)),
            ),
            scratch_shapes=[
                pltpu.VMEM((9, L_DEV + 8, 128), F32),
                pltpu.VMEM((L_DEV, GROUP_CH), BF16),
                pltpu.VMEM((4, L_DEV, OWN_CH), F32),
                pltpu.VMEM((128, GROUP_CH), BF16),
                pltpu.VMEM((128, GROUP_CH), BF16),
            ],
        ),
        out_shape=(
            jax.ShapeDtypeStruct((L_DEV, D_IN), BF16),
            jax.ShapeDtypeStruct((L_DEV, GROUPS * STATE), BF16),
            jax.ShapeDtypeStruct((GROUPS, STATE, GROUP_CH), BF16),
            jax.ShapeDtypeStruct((SHARDS, SENT_ROWS, OWN_CH), BF16),
        ),
        cost_estimate=pl.CostEstimate(flops=10 * 10**9, bytes_accessed=14 * 2**20, transcendentals=0),
        compiler_params=pltpu.CompilerParams(vmem_limit_bytes=VMEM_LIMIT),
        name="conv_state",
    )(mask, rows, rows, before, before, weight, weight, bias, bias, rows, cols)


def intra_kernel(
    x_ref, b_ref, c_ref, hc_ref, wc_ref, bc_ref, row_ref, col_ref, y_ref, co_ref, cf
):
    half = BLOCK // 2
    j = pl.program_id(1)
    sums = pltpu.roll(col_ref[...], (GROUPS - pl.program_id(0)) * PER_GROUP, 1)

    @pl.when(j == 0)
    def _():
        cf[5:8, :] = hc_ref[0].astype(F32)

    @pl.when(j == 1)
    def _():
        cf[0:8, :] = cf[BLOCK : BLOCK + 8, :]

    cf[8 : 8 + BLOCK, :] = c_ref[0].astype(F32)
    w, bias = taps(wc_ref, bc_ref, slice(0, 128))
    for r0 in range(0, BLOCK, CONV_ROWS):
        co_ref[r0 : r0 + CONV_ROWS, :] = silu_of(cf, 5 + r0, w, bias).astype(BF16)
    scores = lax.dot_general(
        co_ref[...], b_ref[...], (((1,), (1,)), ((), ())), preferred_element_type=F32
    )
    t = lax.broadcasted_iota(jnp.int32, (half, half), 0)
    u = lax.broadcasted_iota(jnp.int32, (half, half), 1)
    s00 = jnp.where(u <= t, scores[:half, :half], 0.0)
    s10 = scores[half:, :half]
    s11 = jnp.where(u <= t, scores[half:, half:], 0.0)
    low = lax.broadcasted_iota(jnp.int32, (BLOCK, 128), 1) < HEAD_DIM
    for pair in range(PER_GROUP // 2):
        lanes = slice(pair * 128, (pair + 1) * 128)
        x = x_ref[:, lanes]
        zero = jnp.zeros_like(x)
        xl, xh = jnp.where(low, x, zero), jnp.where(low, zero, x)
        top, bottom = [], []
        for h in (2 * pair, 2 * pair + 1):
            cs0 = jnp.broadcast_to(sums[:half, h : h + 1], (half, half))
            cs1 = jnp.broadcast_to(sums[half:, h : h + 1], (half, half))
            a0 = row_ref[h : h + 1, :half]
            a1 = row_ref[h : h + 1, half:]
            top.append((jnp.exp2(jnp.minimum(cs0 - a0, CAP)) * s00).astype(BF16))
            bottom.append((jnp.exp2(cs1 - a0) * s10).astype(BF16))
            bottom.append((jnp.exp2(jnp.minimum(cs1 - a1, CAP)) * s11).astype(BF16))
        above = dot(jnp.concatenate(top, axis=1), jnp.concatenate([xl[:half], xh[:half]], axis=0))
        below = dot(jnp.concatenate(bottom, axis=1), jnp.concatenate([xl, xh], axis=0))
        y_ref[:half, lanes] = above.astype(BF16)
        y_ref[half:, lanes] = below.astype(BF16)


def intra(x, b, rows, before, weight, bias, starts, sums):
    def at_c(g, j):
        return (0, D_IN // 128 + GROUPS + g)

    return pl.pallas_call(
        intra_kernel,
        grid=(GROUPS, L_DEV // BLOCK),
        in_specs=[
            pl.BlockSpec((BLOCK, GROUP_CH), lambda g, j: (j, g)),
            pl.BlockSpec((BLOCK, 128), lambda g, j: (j, g)),
            pl.BlockSpec((1, BLOCK, 128), lambda g, j: (0, j, at_c(g, j)[1])),
            pl.BlockSpec((1, 3, 128), lambda g, j: (0, 0, at_c(g, j)[1])),
            pl.BlockSpec((4, 128), at_c),
            pl.BlockSpec((1, 128), at_c),
            pl.BlockSpec((PER_GROUP, BLOCK), lambda g, j: (g, j)),
            pl.BlockSpec((BLOCK, 2 * HEADS), lambda g, j: (j, 0)),
        ],
        out_specs=(
            pl.BlockSpec((BLOCK, GROUP_CH), lambda g, j: (j, g)),
            pl.BlockSpec((BLOCK, 128), lambda g, j: (j, g)),
        ),
        out_shape=(
            jax.ShapeDtypeStruct((L_DEV, D_IN), BF16),
            jax.ShapeDtypeStruct((L_DEV, GROUPS * STATE), BF16),
        ),
        scratch_shapes=[pltpu.VMEM((BLOCK + 8, 128), F32)],
        cost_estimate=pl.CostEstimate(flops=12 * 10**9, bytes_accessed=12 * 2**20, transcendentals=0),
        compiler_params=pltpu.CompilerParams(vmem_limit_bytes=VMEM_LIMIT),
        name="intra",
    )(x, b, rows, before, weight, bias, starts, sums)


def scan_kernel(r_ref, p_ref, piece_ref):
    state = jnp.zeros((STATE, OWN_CH), F32)
    for d in range(SHARDS):
        slot = d ^ FLIP
        p_ref[slot] = state.astype(BF16)
        extra = r_ref[slot, STATE:, :].astype(F32)
        state = (extra[0:1] + extra[1:2]) * state + r_ref[slot, :STATE, :].astype(F32)
    size = STATE // PIECES
    zero = jnp.zeros((PIECE_ROWS - size - 3, OWN_CH), F32)
    for k in range(PIECES):
        rows = extra[2 + 2 * k : 4 + 2 * k]
        parts = [state[k * size : k * size + size], rows, extra[6 + k : 7 + k], zero]
        piece_ref[k * PIECE_ROWS : (k + 1) * PIECE_ROWS, :] = jnp.concatenate(parts, axis=0).astype(BF16)


def scan(got):
    return pl.pallas_call(
        scan_kernel,
        out_shape=(
            jax.ShapeDtypeStruct((SHARDS, STATE, OWN_CH), BF16),
            jax.ShapeDtypeStruct((PIECES * PIECE_ROWS, OWN_CH), BF16),
        ),
        cost_estimate=pl.CostEstimate(flops=10**9, bytes_accessed=2**22, transcendentals=0),
        compiler_params=pltpu.CompilerParams(vmem_limit_bytes=VMEM_LIMIT),
        name="scan",
    )(got)


def pack_kernel(place_ref, prompt_ref, owner_ref, *refs):
    pieces, p_ref = refs[:-1], refs[-1]
    p_ref[...] = jnp.zeros_like(p_ref)
    for k in range(PIECES):
        p_ref[owner_ref[place_ref[0] ^ prompt_ref[0] ^ k] ^ FLIP] = pieces[k][...]


def pack(place, prompt, owner_slot, pieces):
    return pl.pallas_call(
        pack_kernel,
        in_specs=[SMEM] * 3 + [VMEM] * PIECES,
        out_shape=jax.ShapeDtypeStruct((SHARDS, PIECE_ROWS, OWN_CH), BF16),
        cost_estimate=pl.CostEstimate(flops=10**8, bytes_accessed=2**19, transcendentals=0),
        compiler_params=pltpu.CompilerParams(vmem_limit_bytes=VMEM_LIMIT),
        name="pack",
    )(place, prompt, owner_slot, *pieces)


def unpack_kernel(place_ref, prompt_ref, owner_ref, r_ref, ssm_ref, conv_ref):
    size = STATE // PIECES
    mine = 0
    for p in range(SHARDS):
        mine = jnp.where(owner_ref[p] == place_ref[0], p, mine)
    parts = [r_ref[mine ^ prompt_ref[0] ^ k ^ FLIP].astype(F32) for k in range(PIECES)]
    state = jnp.concatenate([part[:size] for part in parts], axis=0)
    ssm_ref[...] = jnp.transpose(state)
    rows = jnp.concatenate([part[size : size + 2] for part in parts], axis=0)
    ends = [part[size + 2 : size + 3, n * 128 : n * 128 + 128] for part in parts for n in range(2)]
    window = jnp.concatenate([rows, jnp.concatenate(ends, axis=0)], axis=1)
    moved = jnp.concatenate([window[:, 64:], window[:, :64]], axis=1)
    odd = prompt_ref[0] % 2 == 1
    conv_ref[...] = jnp.where(odd, moved, window)[:, : CH // SHARDS].astype(BF16)


def unpack(place, prompt, owner_slot, got):
    return pl.pallas_call(
        unpack_kernel,
        in_specs=[SMEM] * 3 + [VMEM],
        out_shape=(
            jax.ShapeDtypeStruct((OWN_CH, STATE), F32),
            jax.ShapeDtypeStruct((4, CH // SHARDS), BF16),
        ),
        cost_estimate=pl.CostEstimate(flops=10**8, bytes_accessed=2**19, transcendentals=0),
        compiler_params=pltpu.CompilerParams(vmem_limit_bytes=VMEM_LIMIT),
        name="unpack",
    )(place, prompt, owner_slot, got)


def out_kernel(mask_ref, y_ref, c_ref, col_ref, e0_ref, state_ref, gain_ref, o_ref, ys, spread):
    within = mask_ref[0] % 4

    @pl.when(pl.program_id(0) == 0)
    def _():
        spread[...] = spread_matrix(GROWN)

    decay = dot(col_ref[0, 240:256, :], spread[...])[15:16]
    for j in range(2):
        rows = slice(j * BLOCK, (j + 1) * BLOCK)
        c = c_ref[rows, :]
        grown = col_ref[0, rows, :]
        total = jnp.zeros((BLOCK, 128), F32)
        for s in range(4):
            lanes = slice(s * OWN_CH, (s + 1) * OWN_CH)
            state = state_ref[s ^ within]
            if j == 1:
                state = (decay[:, lanes] * state.astype(F32) + e0_ref[0, :, lanes].astype(F32)).astype(BF16)
            y = y_ref[rows, lanes].astype(F32) + dot(grown, spread[:, lanes]) * dot(c, state)
            ys[:, lanes] = y
            total = total + y[:, :128] * y[:, :128] + y[:, 128:] * y[:, 128:]
        mean = jnp.sum(total, axis=1, keepdims=True) * (1.0 / GROUP_CH)
        scale = lax.rsqrt(mean + NORM_EPS)
        o_ref[0, rows, :] = (ys[...] * scale * gain_ref[...]).astype(BF16)


def finish(y, c, cols, e0, states, gain, mask):
    return pl.pallas_call(
        out_kernel,
        grid_spec=pltpu.PrefetchScalarGridSpec(
            num_scalar_prefetch=1,
            grid=(GROUPS,),
            in_specs=[
                pl.BlockSpec((L_DEV, GROUP_CH), lambda g, m: (0, g)),
                pl.BlockSpec((L_DEV, 128), lambda g, m: (0, g)),
                pl.BlockSpec((1, L_DEV, 128), lambda g, m: (g, 0, 0)),
                pl.BlockSpec((1, STATE, GROUP_CH), lambda g, m: (g, 0, 0)),
                pl.BlockSpec((4, STATE, OWN_CH), lambda g, m: (g ^ (m[0] // 4), 0, 0)),
                pl.BlockSpec((1, GROUP_CH), lambda g, m: (0, g)),
            ],
            out_specs=pl.BlockSpec((1, L_DEV, GROUP_CH), lambda g, m: (0, 0, g)),
            scratch_shapes=[pltpu.VMEM((BLOCK, GROUP_CH), F32), pltpu.VMEM((128, GROUP_CH), BF16)],
        ),
        out_shape=jax.ShapeDtypeStruct((1, L_DEV, D_IN), BF16),
        cost_estimate=pl.CostEstimate(flops=8 * 10**9, bytes_accessed=12 * 2**20, transcendentals=0),
        compiler_params=pltpu.CompilerParams(vmem_limit_bytes=VMEM_LIMIT),
        name="finish",
    )(mask, y, c, cols, e0, states, gain)


def exchange(pieces):
    groups = [[(r ^ FLIP) * SHARDS + p for r in range(SHARDS)] for p in range(SHARDS)]
    return lax.all_to_all(
        pieces, ("seq", "grp"), split_axis=0, concat_axis=0, tiled=True, axis_index_groups=groups
    )


def body(conv_input, step_raw, decay_rate, conv_weight, conv_bias, norm_gain, owner_slot):
    place = lax.axis_index("seq").astype(jnp.int32)[None]
    prompt = lax.axis_index("grp").astype(jnp.int32)[None]
    route = [(d, d + 1) for d in range(SHARDS - 1)]
    before = lax.ppermute(conv_input[:, L_DEV - 3 :, :], "seq", route)
    starts, sums, cols = prep(step_raw, decay_rate[None, :])
    bias = conv_bias[None, :]
    x, b, e0, sent = conv(conv_input, before, conv_weight, bias, cols, prompt ^ FLIP)
    y, c = intra(x, b, conv_input, before, conv_weight, bias, starts, sums)
    got, y = lax.optimization_barrier((exchange(sent), y))
    states, final = scan(got)
    entering = exchange(states)
    turn = [
        (r * SHARDS + p, r * SHARDS + (r ^ p)) for r in range(SHARDS) for p in range(SHARDS)
    ]
    final = lax.ppermute(final, ("seq", "grp"), turn)
    kept, passed = final[:PIECE_ROWS], final[PIECE_ROWS:]
    pieces = [kept, lax.ppermute(passed, "seq", [(r, r ^ 1) for r in range(SHARDS)])]
    packed = pack(place, prompt, owner_slot, pieces)
    entering, packed = lax.optimization_barrier((entering, packed))
    arrived = exchange(packed)
    mixed = finish(y, c, cols, e0, entering, norm_gain[None, :], prompt ^ FLIP)
    ssm, rows = unpack(place, prompt, owner_slot, arrived)
    return mixed, ssm.reshape(1, 4, HEAD_DIM, STATE), jnp.transpose(rows)[None]


def solution(mesh):
    return jax.shard_map(
        body,
        mesh=mesh,
        in_specs=(P("grp", "seq", None), P("grp", None, "seq"), P(), P(), P(), P(), P()),
        out_specs=(P("grp", "seq", None), P("seq", "grp", None, None), P("seq", "grp", None)),
        check_vma=False,
    )
```

time: 92.8 us -> 86 us (0.927)
  waiting for transfers between devices: 18 us -> 4.92 us
  starting transfers between devices: 31.4 us -> 39.1 us
  Pallas kernels: 38.9 us -> 36.7 us
    all_to_all x3, waiting for transfers between devices: 9.37 us -> 1.39 us  [exchange(): lax.all_to_all(pieces, ('seq', 'grp'), split_axis=0, concat_axis=0, tiled...]
    all_to_all x3, starting transfers between devices: 20.5 us -> 27.8 us  [exchange(): lax.all_to_all(pieces, ('seq', 'grp'), split_axis=0, concat_axis=0, tiled...]
    ppermute x2, waiting for transfers between devices: 8.65 us -> 3.53 us  [the longest x1 3.53 us: body(): lax.ppermute(passed, 'seq', [(r, r ^ 1) for r in range(SHARDS)])]
    pallas_call x1, Pallas kernels: 11.6 us -> 9.78 us  [conv(): pl.pallas_call(conv_kernel, grid_spec=pltpu.PrefetchScalarGridSpec(num_sc...]
  transfers between devices with their start and end apart: 6 -> 6, of which waited for: 3 -> 2; matrix products, arithmetic and copies ran while one was open for 1% -> 2% of each run, Pallas kernels for 25% -> 27%
where the time goes in v2:
time: 86 us; the launch traced here: 84.9 us
  starting transfers between devices  39.1 us (45%)
  Pallas kernels  36.7 us (43%)
  waiting for transfers between devices  4.92 us (6%)
  local copies, waits for them, and re-layouts  3.46 us (4%)
    all_to_all x3, starting transfers between devices, exchange(): lax.all_to_all(pieces, ('seq', 'grp'), split_axis=0, concat_axis=0, tiled...  27.8 us
    pallas_call x1, Pallas kernels, intra(): pl.pallas_call(intra_kernel, grid=(GROUPS, L_DEV // BLOCK), in_specs=[pl....  11.3 us
    pallas_call x1, Pallas kernels, conv(): pl.pallas_call(conv_kernel, grid_spec=pltpu.PrefetchScalarGridSpec(num_sc...  9.78 us
    pallas_call x1, Pallas kernels, finish(): pl.pallas_call(out_kernel, grid_spec=pltpu.PrefetchScalarGridSpec(num_sca...  7.4 us
    ppermute x1, starting transfers between devices, body(): lax.ppermute(passed, 'seq', [(r, r ^ 1) for r in range(SHARDS)])  5.23 us
    ppermute x1, starting transfers between devices, body(): before = lax.ppermute(conv_input[:, L_DEV - 3:, :], 'seq', route)  4.53 us
    ppermute x1, waiting for transfers between devices, body(): lax.ppermute(passed, 'seq', [(r, r ^ 1) for r in range(SHARDS)])  3.53 us
    pallas_call x1, Pallas kernels, scan(): pl.pallas_call(scan_kernel, out_shape=(jax.ShapeDtypeStruct((SHARDS, STAT...  2.46 us
  transfers between devices with their start and end apart: 6, of which 2 were waited for; matrix products, arithmetic and copies ran while one was open for 2% of the time, Pallas kernels for 27%

profile of v2, /device:TPU:1, one launch (start us, length us, event | category | flops | bytes accessed | tf_op | source)
XLA Modules:
  0.0 84.9 jit_solution(15753754323778071961)
XLA Ops:
  0.6 1.5 %slice.9 = bf16[1,3,5120]{2,1,0:T(4,128)(2,1)} slice(bf16[1,512,5120]{2,1,0:T(8,128)(2,1)} %c_ref.1), slice={[0:1], [509:512], [0:5120]} | slice | bytes 61440 | tf_op jit(solution)/shard_map/slice | solution.py:438
  2.2 4.5 %collective-permute-start = (bf16[1,3,5120]{2,1,0:T(4,128)(2,1)}, bf16[1,3,5120]{2,1,0:T(4,128)(2,1)}, u32[]{:S(2)}, u32[]{:S(2)}) collective-permute-start(bf16[1,3,5120]{2,1,0:T(4,128)(2,1)} %slice.9), channel_id=1, source_target_pairs={{0,16},{16,32},{32,48},{48,64},{64,80},{80,96},{96,112},{112,128},... | collective-permute-start | bytes 92168 | tf_op jit(solution)/shard_map/ppermute | solution.py:438
  6.7 2.3 %prep.1 = (f32[64,512]{1,0:T(8,128)}, f32[512,128]{1,0:T(8,128)}, bf16[4,512,128]{2,1,0:T(8,128)(2,1)}) custom-call(f32[1,64,512]{2,1,0:T(8,128)} %step_ref.1, f32[1,64]{1,0:T(1,128)} %bitcast.11), custom_call_target="tpu_custom_call" | custom-call | flops 1000000000 | bytes 2097152 | tf_op jit(solution)/shard_map/prep/pallas_call | solution.py:88
  9.0 1.3 %broadcast_in_dim.19.bx_ref.bb_ref.bc_ref = bf16[1,5120]{1,0:T(2,128)(2,1)} reshape(bf16[5120]{0:T(1024)(128)(2,1)} %param.11) | data formatting | bytes 20480 | tf_op jit(solution)/shard_map/broadcast_in_dim | solution.py:440
  10.3 0.0 collective-permute-done.hx_ref.hb_ref.hc_ref
  10.3 9.8 %conv_state.1 = (bf16[512,4096]{1,0:T(8,128)(2,1)}, bf16[512,512]{1,0:T(8,128)(2,1)}, bf16[4,128,1024]{2,1,0:T(8,128)(2,1)}, bf16[16,136,256]{2,1,0:T(8,128)(2,1)}) custom-call(s32[1]{0:T(128)S(6)} %xor.4.mask_ref, bf16[1,512,5120]{2,1,0:T(8,128)(2,1)} %c_ref.1, bf16[1,512,5120]{2,1,0:T(8,128)(2,1)} %c_ref.1, ...), custom_call_target="tpu_custom_call" | custom-call | flops 10000000000 | bytes 14680064 | tf_op jit(solution)/shard_map/conv_state/pallas_call | solution.py:182
  20.1 7.4 %all-to-all-start = ((bf16[16,136,256]{2,1,0:T(8,128)(2,1)}), bf16[16,136,256]{2,1,0:T(8,128)(2,1)}, u32[]{:S(2)}, u32[]{:S(2)}) async-start(bf16[16,136,256]{2,1,0:T(8,128)(2,1)} %get-tuple-element.21), calls=%async_computation | async-start | bytes 2228224 | tf_op jit(solution)/shard_map/all_to_all | solution.py:429
  27.5 11.3 %intra.1 = (bf16[512,4096]{1,0:T(8,128)(2,1)}, bf16[512,512]{1,0:T(8,128)(2,1)}) custom-call(bf16[512,4096]{1,0:T(8,128)(2,1)} %get-tuple-element.22.x_ref, bf16[512,512]{1,0:T(8,128)(2,1)} %get-tuple-element.23.b_ref, bf16[1,512,5120]{2,1,0:T(8,128)(2,1)} %c_ref.1, bf16[1,3,5120]{2,1,0:T(4,128)(2,1)} %collective-permute-done.hx_ref.hb_ref.hc_ref, ...), custom_call_target="tpu_custom_call" | custom-call | flops 12000000000 | bytes 12582912 | tf_op jit(solution)/shard_map/intra/pallas_call | solution.py:273
  38.8 1.4 %all-to-all-done.r_ref = bf16[16,136,256]{2,1,0:T(8,128)(2,1)} async-done(((bf16[16,136,256]{2,1,0:T(8,128)(2,1)}), bf16[16,136,256]{2,1,0:T(8,128)(2,1)}, u32[]{:S(2)}, u32[]{:S(2)}) %all-to-all-start) | async-done | bytes 1114144 | tf_op jit(solution)/shard_map/all_to_all | solution.py:429
  40.2 2.5 %scan.1 = (bf16[16,128,256]{2,1,0:T(8,128)(2,1)}, bf16[144,256]{1,0:T(8,128)(2,1)}) custom-call(bf16[16,136,256]{2,1,0:T(8,128)(2,1)} %all-to-all-done.r_ref), custom_call_target="tpu_custom_call" | custom-call | flops 1000000000 | bytes 4194304 | tf_op jit(solution)/shard_map/scan/pallas_call | solution.py:317
  42.7 8.0 %all-to-all-start.1 = ((bf16[16,128,256]{2,1,0:T(8,128)(2,1)}), bf16[16,128,256]{2,1,0:T(8,128)(2,1)}, u32[]{:S(2)}, u32[]{:S(2)}) async-start(bf16[16,128,256]{2,1,0:T(8,128)(2,1)} %get-tuple-element.31), calls=%async_computation.1 | async-start | bytes 2097152 | tf_op jit(solution)/shard_map/all_to_all | solution.py:429
  50.7 1.5 %collective-permute-start.1 = (bf16[144,256]{1,0:T(8,128)(2,1)}, bf16[144,256]{1,0:T(8,128)(2,1)S(1)}, u32[]{:S(2)}, u32[]{:S(2)}) collective-permute-start(bf16[144,256]{1,0:T(8,128)(2,1)} %get-tuple-element.32), channel_id=1, source_target_pairs={{0,0},{1,1},{2,2},{3,3},{4,4},{5,5},{6,6},{7,7},{8,8},{9,9},{10,10... | collective-permute-start | bytes 221192 | tf_op jit(solution)/shard_map/ppermute | solution.py:449
  52.2 0.0 collective-permute-done.1
  52.2 0.6 fusion
  52.8 5.2 %collective-permute-start.2 = (bf16[72,256]{1,0:T(8,128)(2,1)S(1)}, bf16[72,256]{1,0:T(8,128)(2,1)}, u32[]{:S(2)}, u32[]{:S(2)}) collective-permute-start(bf16[72,256]{1,0:T(8,128)(2,1)S(1)} %get-tuple-element.37), channel_id=1, source_target_pairs={{0,16},{16,0},{32,48},{48,32},{64,80},{80,64},{96,112},{112,96},{1... | collective-permute-start | bytes 110600 | tf_op jit(solution)/shard_map/ppermute | solution.py:451
  58.1 3.5 %collective-permute-done.2.refs_1_ = bf16[72,256]{1,0:T(8,128)(2,1)} collective-permute-done((bf16[72,256]{1,0:T(8,128)(2,1)S(1)}, bf16[72,256]{1,0:T(8,128)(2,1)}, u32[]{:S(2)}, u32[]{:S(2)}) %collective-permute-start.2) | collective-permute-done | bytes 36896 | tf_op jit(solution)/shard_map/ppermute | solution.py:451
  61.6 1.7 %pack.1 = bf16[16,72,256]{2,1,0:T(8,128)(2,1)} custom-call(s32[1]{0:T(128)} %bitcast.2.place_ref, s32[1]{0:T(128)} %bitcast.prompt_ref, s32[16]{0:T(128)} %owner_ref.3, bf16[72,256]{1,0:T(8,128)(2,1)} %get-tuple-element.38.refs_0_, bf16[72,256]{1,0:T(8,128)(2,1)} %collective-permute-done.2.refs_1_), custom_call_target="tpu_custom_call" | custom-call | flops 100000000 | bytes 524288 | tf_op jit(solution)/shard_map/pack/pallas_call | solution.py:337
  63.3 0.0 all-to-all-done.1.state_ref
  63.3 12.3 %all-to-all-start.2 = ((bf16[16,72,256]{2,1,0:T(8,128)(2,1)}), bf16[16,72,256]{2,1,0:T(8,128)(2,1)}, u32[]{:S(2)}, u32[]{:S(2)}) async-start(bf16[16,72,256]{2,1,0:T(8,128)(2,1)} %pack.1), calls=%async_computation.2 | async-start | bytes 1179648 | tf_op jit(solution)/shard_map/all_to_all | solution.py:429
  75.6 7.4 %finish.1 = bf16[1,512,4096]{2,1,0:T(8,128)(2,1)} custom-call(s32[1]{0:T(128)S(6)} %xor.4.mask_ref, bf16[512,4096]{1,0:T(8,128)(2,1)} %get-tuple-element.27.y_ref, bf16[512,512]{1,0:T(8,128)(2,1)} %get-tuple-element.28.c_ref, bf16[4,512,128]{2,1,0:T(8,128)(2,1)} %get-tuple-element.20.col_ref, bf16[4,128,1024]{2,1,0:T(8,128)(2,1)} %get-tuple-element.29.e0_ref, ...), custom_call_target="tpu_custom_call" | custom-call | flops 8000000000 | bytes 12582912 | tf_op jit(solution)/shard_map/finish/pallas_call | solution.py:404
  83.0 0.0 all-to-all-done.2.r_ref
  83.0 1.8 %unpack.1 = (f32[256,128]{1,0:T(8,128)}, bf16[4,320]{1,0:T(4,128)(2,1)}) custom-call(s32[1]{0:T(128)} %bitcast.2.place_ref, s32[1]{0:T(128)} %bitcast.prompt_ref, s32[16]{0:T(128)} %owner_ref.3, bf16[16,72,256]{2,1,0:T(8,128)(2,1)} %all-to-all-done.2.r_ref), custom_call_target="tpu_custom_call" | custom-call | flops 100000000 | bytes 524288 | tf_op jit(solution)/shard_map/unpack/pallas_call | solution.py:364
Async XLA Ops:
  2.2 8.1 %collective-permute-start = (bf16[1,3,5120]{2,1,0:T(4,128)(2,1)}, bf16[1,3,5120]{2,1,0:T(4,128)(2,1)}, u32[]{:S(2)}, u32[]{:S(2)}) collective-permute-start(bf16[1,3,5120]{2,1,0:T(4,128)(2,1)} %slice.9), channel_id=1, source_target_pairs={{0,16},{16,32},{32,48},{48,64},{64,80},{80,96},{96,112},{112,128},... | collective-permute-start | bytes 92168 | tf_op jit(solution)/shard_map/ppermute | solution.py:438
  20.1 20.1 %all-to-all-start = ((bf16[16,136,256]{2,1,0:T(8,128)(2,1)}), bf16[16,136,256]{2,1,0:T(8,128)(2,1)}, u32[]{:S(2)}, u32[]{:S(2)}) async-start(bf16[16,136,256]{2,1,0:T(8,128)(2,1)} %get-tuple-element.21), calls=%async_computation | async-start | bytes 2228224 | tf_op jit(solution)/shard_map/all_to_all | solution.py:429
  42.7 20.6 %all-to-all-start.1 = ((bf16[16,128,256]{2,1,0:T(8,128)(2,1)}), bf16[16,128,256]{2,1,0:T(8,128)(2,1)}, u32[]{:S(2)}, u32[]{:S(2)}) async-start(bf16[16,128,256]{2,1,0:T(8,128)(2,1)} %get-tuple-element.31), calls=%async_computation.1 | async-start | bytes 2097152 | tf_op jit(solution)/shard_map/all_to_all | solution.py:429
  50.7 1.5 %collective-permute-start.1 = (bf16[144,256]{1,0:T(8,128)(2,1)}, bf16[144,256]{1,0:T(8,128)(2,1)S(1)}, u32[]{:S(2)}, u32[]{:S(2)}) collective-permute-start(bf16[144,256]{1,0:T(8,128)(2,1)} %get-tuple-element.32), channel_id=1, source_target_pairs={{0,0},{1,1},{2,2},{3,3},{4,4},{5,5},{6,6},{7,7},{8,8},{9,9},{10,10... | collective-permute-start | bytes 221192 | tf_op jit(solution)/shard_map/ppermute | solution.py:449
  52.8 8.8 %collective-permute-start.2 = (bf16[72,256]{1,0:T(8,128)(2,1)S(1)}, bf16[72,256]{1,0:T(8,128)(2,1)}, u32[]{:S(2)}, u32[]{:S(2)}) collective-permute-start(bf16[72,256]{1,0:T(8,128)(2,1)S(1)} %get-tuple-element.37), channel_id=1, source_target_pairs={{0,16},{16,0},{32,48},{48,32},{64,80},{80,64},{96,112},{112,96},{1... | collective-permute-start | bytes 110600 | tf_op jit(solution)/shard_map/ppermute | solution.py:451
  63.3 19.7 %all-to-all-start.2 = ((bf16[16,72,256]{2,1,0:T(8,128)(2,1)}), bf16[16,72,256]{2,1,0:T(8,128)(2,1)}, u32[]{:S(2)}, u32[]{:S(2)}) async-start(bf16[16,72,256]{2,1,0:T(8,128)(2,1)} %pack.1), calls=%async_computation.2 | async-start | bytes 1179648 | tf_op jit(solution)/shard_map/all_to_all | solution.py:429

commit v3 on v2

--- a/solution.py
+++ b/solution.py
@@ -138,21 +138,11 @@
     ends = jnp.concatenate([col_ref[0, 240:256, :], col_ref[0, 496:512, :]], axis=0)
     decays = dot(ends, regrown[...])
     last = last_ref[0].astype(F32)[12:16]
-    for s in range(4):
+    def widen(s):
+        tails[s] = dot(col_ref[0], spread[:, s * OWN_CH : (s + 1) * OWN_CH])
+
+    def emit(s):
         wide = slice(s * OWN_CH, (s + 1) * OWN_CH)
-        tails[s] = dot(col_ref[0], spread[:, wide])
-        pair = (2 * s, 2 * s + 1)
-        both = []
-        for k in pair:
-            lanes = slice(k * 128, (k + 1) * 128)
-            load(k, x_ref, hx_ref, lanes)
-            both.append(taps(wx_ref, bx_ref, lanes))
-        for r0 in range(0, L_DEV, CONV_ROWS):
-            rows = slice(r0, r0 + CONV_ROWS)
-            parts = [silu_of(xf.at[k], 5 + r0, *tap) for k, tap in zip(pair, both)]
-            value = jnp.concatenate(parts, axis=1)
-            xo_ref[rows, wide] = value.astype(BF16)
-            xs[rows, wide] = (value * tails[s, rows, :]).astype(BF16)
         first, second = decays[15:16, wide], decays[31:32, wide]
         e0 = dot(bt[0], xs[:BLOCK, wide])
         e1 = dot(bt[1], xs[BLOCK:, wide])
@@ -167,6 +157,27 @@
             jnp.concatenate(ends_of[:2], axis=1), jnp.concatenate(ends_of[2:], axis=1),
         ]
         p_ref[slot, STATE:, :] = jnp.concatenate(extra, axis=0).astype(BF16)
+
+    widen(0)
+    for s in range(4):
+        wide = slice(s * OWN_CH, (s + 1) * OWN_CH)
+        pair = (2 * s, 2 * s + 1)
+        both = []
+        for k in pair:
+            lanes = slice(k * 128, (k + 1) * 128)
+            load(k, x_ref, hx_ref, lanes)
+            both.append(taps(wx_ref, bx_ref, lanes))
+        for r0 in range(0, L_DEV, CONV_ROWS):
+            if r0 == 0 and s < 3:
+                widen(s + 1)
+            if r0 == 0 and s > 0:
+                emit(s - 1)
+            rows = slice(r0, r0 + CONV_ROWS)
+            parts = [silu_of(xf.at[k], 5 + r0, *tap) for k, tap in zip(pair, both)]
+            value = jnp.concatenate(parts, axis=1)
+            xo_ref[rows, wide] = value.astype(BF16)
+            xs[rows, wide] = (value * tails[s, rows, :]).astype(BF16)
+    emit(3)
 
 
 CONV_AT = (0, 256, 640, 896)
@@ -299,14 +310,14 @@
 
 
 def scan_kernel(r_ref, p_ref, piece_ref):
-    state = jnp.zeros((STATE, OWN_CH), F32)
+    state = jnp.zeros((STATE, r_ref.shape[-1]), F32)
     for d in range(SHARDS):
         slot = d ^ FLIP
         p_ref[slot] = state.astype(BF16)
         extra = r_ref[slot, STATE:, :].astype(F32)
         state = (extra[0:1] + extra[1:2]) * state + r_ref[slot, :STATE, :].astype(F32)
     size = STATE // PIECES
-    zero = jnp.zeros((PIECE_ROWS - size - 3, OWN_CH), F32)
+    zero = jnp.zeros((PIECE_ROWS - size - 3, r_ref.shape[-1]), F32)
     for k in range(PIECES):
         rows = extra[2 + 2 * k : 4 + 2 * k]
         parts = [state[k * size : k * size + size], rows, extra[6 + k : 7 + k], zero]
@@ -316,6 +327,12 @@
 def scan(got):
     return pl.pallas_call(
         scan_kernel,
+        grid=(OWN_CH // 128,),
+        in_specs=[pl.BlockSpec((SHARDS, SENT_ROWS, 128), lambda i: (0, 0, i))],
+        out_specs=(
+            pl.BlockSpec((SHARDS, STATE, 128), lambda i: (0, 0, i)),
+            pl.BlockSpec((PIECES * PIECE_ROWS, 128), lambda i: (0, i)),
+        ),
         out_shape=(
             jax.ShapeDtypeStruct((SHARDS, STATE, OWN_CH), BF16),
             jax.ShapeDtypeStruct((PIECES * PIECE_ROWS, OWN_CH), BF16),

time: 86 us -> 85.3 us (level)
  no operation moved by 1% of the time
where the time goes in v3:
time: 85.3 us; the launch traced here: 84.2 us
  starting transfers between devices  39.1 us (46%)
  Pallas kernels  36.1 us (42%)
  waiting for transfers between devices  4.9 us (6%)
  local copies, waits for them, and re-layouts  3.46 us (4%)
    all_to_all x3, starting transfers between devices, exchange(): lax.all_to_all(pieces, ('seq', 'grp'), split_axis=0, concat_axis=0, tiled...  27.8 us
    pallas_call x1, Pallas kernels, intra(): pl.pallas_call(intra_kernel, grid=(GROUPS, L_DEV // BLOCK), in_specs=[pl....  11.3 us
    pallas_call x1, Pallas kernels, conv(): pl.pallas_call(conv_kernel, grid_spec=pltpu.PrefetchScalarGridSpec(num_sc...  9.42 us
    pallas_call x1, Pallas kernels, finish(): pl.pallas_call(out_kernel, grid_spec=pltpu.PrefetchScalarGridSpec(num_sca...  7.4 us
    ppermute x1, starting transfers between devices, body(): lax.ppermute(passed, 'seq', [(r, r ^ 1) for r in range(SHARDS)])  5.24 us
    ppermute x1, starting transfers between devices, body(): before = lax.ppermute(conv_input[:, L_DEV - 3:, :], 'seq', route)  4.53 us
    ppermute x1, waiting for transfers between devices, body(): lax.ppermute(passed, 'seq', [(r, r ^ 1) for r in range(SHARDS)])  3.5 us
    pallas_call x1, Pallas kernels, prep(): pl.pallas_call(prep_kernel, out_shape=(jax.ShapeDtypeStruct((HEADS, L_DEV...  2.29 us
  transfers between devices with their start and end apart: 6, of which 2 were waited for; matrix products, arithmetic and copies ran while one was open for 2% of the time, Pallas kernels for 27%

profile of v3, /device:TPU:1, one launch (start us, length us, event | category | flops | bytes accessed | tf_op | source)
XLA Modules:
  0.0 84.2 jit_solution(889688041236564690)
XLA Ops:
  0.6 1.5 %slice.9 = bf16[1,3,5120]{2,1,0:T(4,128)(2,1)} slice(bf16[1,512,5120]{2,1,0:T(8,128)(2,1)} %c_ref.1), slice={[0:1], [509:512], [0:5120]} | slice | bytes 61440 | tf_op jit(solution)/shard_map/slice | solution.py:455
  2.2 4.5 %collective-permute-start = (bf16[1,3,5120]{2,1,0:T(4,128)(2,1)}, bf16[1,3,5120]{2,1,0:T(4,128)(2,1)}, u32[]{:S(2)}, u32[]{:S(2)}) collective-permute-start(bf16[1,3,5120]{2,1,0:T(4,128)(2,1)} %slice.9), channel_id=1, source_target_pairs={{0,16},{16,32},{32,48},{48,64},{64,80},{80,96},{96,112},{112,128},... | collective-permute-start | bytes 92168 | tf_op jit(solution)/shard_map/ppermute | solution.py:455
  6.7 2.3 %prep.1 = (f32[64,512]{1,0:T(8,128)}, f32[512,128]{1,0:T(8,128)}, bf16[4,512,128]{2,1,0:T(8,128)(2,1)}) custom-call(f32[1,64,512]{2,1,0:T(8,128)} %step_ref.1, f32[1,64]{1,0:T(1,128)} %bitcast.11), custom_call_target="tpu_custom_call" | custom-call | flops 1000000000 | bytes 2097152 | tf_op jit(solution)/shard_map/prep/pallas_call | solution.py:88
  9.0 1.3 %broadcast_in_dim.19.bx_ref.bb_ref.bc_ref = bf16[1,5120]{1,0:T(2,128)(2,1)} reshape(bf16[5120]{0:T(1024)(128)(2,1)} %param.11) | data formatting | bytes 20480 | tf_op jit(solution)/shard_map/broadcast_in_dim | solution.py:457
  10.3 0.0 collective-permute-done.hx_ref.hb_ref.hc_ref
  10.3 9.4 %conv_state.1 = (bf16[512,4096]{1,0:T(8,128)(2,1)}, bf16[512,512]{1,0:T(8,128)(2,1)}, bf16[4,128,1024]{2,1,0:T(8,128)(2,1)}, bf16[16,136,256]{2,1,0:T(8,128)(2,1)}) custom-call(s32[1]{0:T(128)S(6)} %xor.4.mask_ref, bf16[1,512,5120]{2,1,0:T(8,128)(2,1)} %c_ref.1, bf16[1,512,5120]{2,1,0:T(8,128)(2,1)} %c_ref.1, ...), custom_call_target="tpu_custom_call" | custom-call | flops 10000000000 | bytes 14680064 | tf_op jit(solution)/shard_map/conv_state/pallas_call | solution.py:193
  19.7 7.4 %all-to-all-start = ((bf16[16,136,256]{2,1,0:T(8,128)(2,1)}), bf16[16,136,256]{2,1,0:T(8,128)(2,1)}, u32[]{:S(2)}, u32[]{:S(2)}) async-start(bf16[16,136,256]{2,1,0:T(8,128)(2,1)} %get-tuple-element.21), calls=%async_computation | async-start | bytes 2228224 | tf_op jit(solution)/shard_map/all_to_all | solution.py:446
  27.2 11.3 %intra.1 = (bf16[512,4096]{1,0:T(8,128)(2,1)}, bf16[512,512]{1,0:T(8,128)(2,1)}) custom-call(bf16[512,4096]{1,0:T(8,128)(2,1)} %get-tuple-element.22.x_ref, bf16[512,512]{1,0:T(8,128)(2,1)} %get-tuple-element.23.b_ref, bf16[1,512,5120]{2,1,0:T(8,128)(2,1)} %c_ref.1, bf16[1,3,5120]{2,1,0:T(4,128)(2,1)} %collective-permute-done.hx_ref.hb_ref.hc_ref, ...), custom_call_target="tpu_custom_call" | custom-call | flops 12000000000 | bytes 12582912 | tf_op jit(solution)/shard_map/intra/pallas_call | solution.py:284
  38.5 1.4 %all-to-all-done.r_ref = bf16[16,136,256]{2,1,0:T(8,128)(2,1)} async-done(((bf16[16,136,256]{2,1,0:T(8,128)(2,1)}), bf16[16,136,256]{2,1,0:T(8,128)(2,1)}, u32[]{:S(2)}, u32[]{:S(2)}) %all-to-all-start) | async-done | bytes 1114144 | tf_op jit(solution)/shard_map/all_to_all | solution.py:446
  39.8 2.2 %scan.1 = (bf16[16,128,256]{2,1,0:T(8,128)(2,1)}, bf16[144,256]{1,0:T(8,128)(2,1)}) custom-call(bf16[16,136,256]{2,1,0:T(8,128)(2,1)} %all-to-all-done.r_ref), custom_call_target="tpu_custom_call" | custom-call | flops 1000000000 | bytes 4194304 | tf_op jit(solution)/shard_map/scan/pallas_call | solution.py:328
  42.0 8.0 %all-to-all-start.1 = ((bf16[16,128,256]{2,1,0:T(8,128)(2,1)}), bf16[16,128,256]{2,1,0:T(8,128)(2,1)}, u32[]{:S(2)}, u32[]{:S(2)}) async-start(bf16[16,128,256]{2,1,0:T(8,128)(2,1)} %get-tuple-element.31), calls=%async_computation.1 | async-start | bytes 2097152 | tf_op jit(solution)/shard_map/all_to_all | solution.py:446
  50.0 1.5 %collective-permute-start.1 = (bf16[144,256]{1,0:T(8,128)(2,1)}, bf16[144,256]{1,0:T(8,128)(2,1)S(1)}, u32[]{:S(2)}, u32[]{:S(2)}) collective-permute-start(bf16[144,256]{1,0:T(8,128)(2,1)} %get-tuple-element.32), channel_id=1, source_target_pairs={{0,0},{1,1},{2,2},{3,3},{4,4},{5,5},{6,6},{7,7},{8,8},{9,9},{10,10... | collective-permute-start | bytes 221192 | tf_op jit(solution)/shard_map/ppermute | solution.py:466
  51.5 0.0 collective-permute-done.1
  51.5 0.6 fusion
  52.2 5.2 %collective-permute-start.2 = (bf16[72,256]{1,0:T(8,128)(2,1)S(1)}, bf16[72,256]{1,0:T(8,128)(2,1)}, u32[]{:S(2)}, u32[]{:S(2)}) collective-permute-start(bf16[72,256]{1,0:T(8,128)(2,1)S(1)} %get-tuple-element.37), channel_id=1, source_target_pairs={{0,16},{16,0},{32,48},{48,32},{64,80},{80,64},{96,112},{112,96},{1... | collective-permute-start | bytes 110600 | tf_op jit(solution)/shard_map/ppermute | solution.py:468
  57.4 3.5 %collective-permute-done.2.refs_1_ = bf16[72,256]{1,0:T(8,128)(2,1)} collective-permute-done((bf16[72,256]{1,0:T(8,128)(2,1)S(1)}, bf16[72,256]{1,0:T(8,128)(2,1)}, u32[]{:S(2)}, u32[]{:S(2)}) %collective-permute-start.2) | collective-permute-done | bytes 36896 | tf_op jit(solution)/shard_map/ppermute | solution.py:468
  60.9 1.7 %pack.1 = bf16[16,72,256]{2,1,0:T(8,128)(2,1)} custom-call(s32[1]{0:T(128)} %bitcast.2.place_ref, s32[1]{0:T(128)} %bitcast.prompt_ref, s32[16]{0:T(128)} %owner_ref.3, bf16[72,256]{1,0:T(8,128)(2,1)} %get-tuple-element.38.refs_0_, bf16[72,256]{1,0:T(8,128)(2,1)} %collective-permute-done.2.refs_1_), custom_call_target="tpu_custom_call" | custom-call | flops 100000000 | bytes 524288 | tf_op jit(solution)/shard_map/pack/pallas_call | solution.py:354
  62.6 0.0 all-to-all-done.1.state_ref
  62.6 12.3 %all-to-all-start.2 = ((bf16[16,72,256]{2,1,0:T(8,128)(2,1)}), bf16[16,72,256]{2,1,0:T(8,128)(2,1)}, u32[]{:S(2)}, u32[]{:S(2)}) async-start(bf16[16,72,256]{2,1,0:T(8,128)(2,1)} %pack.1), calls=%async_computation.2 | async-start | bytes 1179648 | tf_op jit(solution)/shard_map/all_to_all | solution.py:446
  74.9 7.4 %finish.1 = bf16[1,512,4096]{2,1,0:T(8,128)(2,1)} custom-call(s32[1]{0:T(128)S(6)} %xor.4.mask_ref, bf16[512,4096]{1,0:T(8,128)(2,1)} %get-tuple-element.27.y_ref, bf16[512,512]{1,0:T(8,128)(2,1)} %get-tuple-element.28.c_ref, bf16[4,512,128]{2,1,0:T(8,128)(2,1)} %get-tuple-element.20.col_ref, bf16[4,128,1024]{2,1,0:T(8,128)(2,1)} %get-tuple-element.29.e0_ref, ...), custom_call_target="tpu_custom_call" | custom-call | flops 8000000000 | bytes 12582912 | tf_op jit(solution)/shard_map/finish/pallas_call | solution.py:421
  82.3 0.0 all-to-all-done.2.r_ref
  82.3 1.9 %unpack.1 = (f32[256,128]{1,0:T(8,128)}, bf16[4,320]{1,0:T(4,128)(2,1)}) custom-call(s32[1]{0:T(128)} %bitcast.2.place_ref, s32[1]{0:T(128)} %bitcast.prompt_ref, s32[16]{0:T(128)} %owner_ref.3, bf16[16,72,256]{2,1,0:T(8,128)(2,1)} %all-to-all-done.2.r_ref), custom_call_target="tpu_custom_call" | custom-call | flops 100000000 | bytes 524288 | tf_op jit(solution)/shard_map/unpack/pallas_call | solution.py:381
Async XLA Ops:
  2.2 8.1 %collective-permute-start = (bf16[1,3,5120]{2,1,0:T(4,128)(2,1)}, bf16[1,3,5120]{2,1,0:T(4,128)(2,1)}, u32[]{:S(2)}, u32[]{:S(2)}) collective-permute-start(bf16[1,3,5120]{2,1,0:T(4,128)(2,1)} %slice.9), channel_id=1, source_target_pairs={{0,16},{16,32},{32,48},{48,64},{64,80},{80,96},{96,112},{112,128},... | collective-permute-start | bytes 92168 | tf_op jit(solution)/shard_map/ppermute | solution.py:455
  19.7 20.1 %all-to-all-start = ((bf16[16,136,256]{2,1,0:T(8,128)(2,1)}), bf16[16,136,256]{2,1,0:T(8,128)(2,1)}, u32[]{:S(2)}, u32[]{:S(2)}) async-start(bf16[16,136,256]{2,1,0:T(8,128)(2,1)} %get-tuple-element.21), calls=%async_computation | async-start | bytes 2228224 | tf_op jit(solution)/shard_map/all_to_all | solution.py:446
  42.0 20.6 %all-to-all-start.1 = ((bf16[16,128,256]{2,1,0:T(8,128)(2,1)}), bf16[16,128,256]{2,1,0:T(8,128)(2,1)}, u32[]{:S(2)}, u32[]{:S(2)}) async-start(bf16[16,128,256]{2,1,0:T(8,128)(2,1)} %get-tuple-element.31), calls=%async_computation.1 | async-start | bytes 2097152 | tf_op jit(solution)/shard_map/all_to_all | solution.py:446
  50.0 1.5 %collective-permute-start.1 = (bf16[144,256]{1,0:T(8,128)(2,1)}, bf16[144,256]{1,0:T(8,128)(2,1)S(1)}, u32[]{:S(2)}, u32[]{:S(2)}) collective-permute-start(bf16[144,256]{1,0:T(8,128)(2,1)} %get-tuple-element.32), channel_id=1, source_target_pairs={{0,0},{1,1},{2,2},{3,3},{4,4},{5,5},{6,6},{7,7},{8,8},{9,9},{10,10... | collective-permute-start | bytes 221192 | tf_op jit(solution)/shard_map/ppermute | solution.py:466
  52.2 8.7 %collective-permute-start.2 = (bf16[72,256]{1,0:T(8,128)(2,1)S(1)}, bf16[72,256]{1,0:T(8,128)(2,1)}, u32[]{:S(2)}, u32[]{:S(2)}) collective-permute-start(bf16[72,256]{1,0:T(8,128)(2,1)S(1)} %get-tuple-element.37), channel_id=1, source_target_pairs={{0,16},{16,0},{32,48},{48,32},{64,80},{80,64},{96,112},{112,96},{1... | collective-permute-start | bytes 110600 | tf_op jit(solution)/shard_map/ppermute | solution.py:468
  62.6 19.7 %all-to-all-start.2 = ((bf16[16,72,256]{2,1,0:T(8,128)(2,1)}), bf16[16,72,256]{2,1,0:T(8,128)(2,1)}, u32[]{:S(2)}, u32[]{:S(2)}) async-start(bf16[16,72,256]{2,1,0:T(8,128)(2,1)} %pack.1), calls=%async_computation.2 | async-start | bytes 1179648 | tf_op jit(solution)/shard_map/all_to_all | solution.py:446

commit v4 on v3

--- a/solution.py
+++ b/solution.py
@@ -128,19 +128,13 @@
         xf[slot, 5:8, :] = halo_ref[0, :, lanes].astype(F32)
         xf[slot, 8 : 8 + L_DEV, :] = ref[0, :, lanes].astype(F32)
 
-    load(8, b_ref, hb_ref, slice(0, 128))
-    w, bias = taps(wb_ref, bb_ref, slice(0, 128))
-    for r0 in range(0, L_DEV, CONV_ROWS):
-        bo_ref[r0 : r0 + CONV_ROWS, :] = silu_of(xf.at[8], 5 + r0, w, bias).astype(BF16)
-    bt = [
-        jnp.transpose(bo_ref[j * BLOCK : (j + 1) * BLOCK, :].astype(F32)).astype(BF16) for j in range(2)
-    ]
+    def widen(s):
+        tails[s] = dot(col_ref[0], spread[:, s * OWN_CH : (s + 1) * OWN_CH])
+
+    widen(0)
     ends = jnp.concatenate([col_ref[0, 240:256, :], col_ref[0, 496:512, :]], axis=0)
     decays = dot(ends, regrown[...])
     last = last_ref[0].astype(F32)[12:16]
-    def widen(s):
-        tails[s] = dot(col_ref[0], spread[:, s * OWN_CH : (s + 1) * OWN_CH])
-
     def emit(s):
         wide = slice(s * OWN_CH, (s + 1) * OWN_CH)
         first, second = decays[15:16, wide], decays[31:32, wide]
@@ -158,7 +152,6 @@
         ]
         p_ref[slot, STATE:, :] = jnp.concatenate(extra, axis=0).astype(BF16)
 
-    widen(0)
     for s in range(4):
         wide = slice(s * OWN_CH, (s + 1) * OWN_CH)
         pair = (2 * s, 2 * s + 1)
@@ -170,6 +163,14 @@
         for r0 in range(0, L_DEV, CONV_ROWS):
             if r0 == 0 and s < 3:
                 widen(s + 1)
+            if r0 == 256 and s == 0:
+                load(8, b_ref, hb_ref, slice(0, 128))
+                w, bias = taps(wb_ref, bb_ref, slice(0, 128))
+                for q in range(0, L_DEV, CONV_ROWS):
+                    bo_ref[q : q + CONV_ROWS, :] = silu_of(xf.at[8], 5 + q, w, bias).astype(BF16)
+                bt = [
+                    jnp.transpose(bo_ref[j * BLOCK : (j + 1) * BLOCK, :].astype(F32)).astype(BF16) for j in range(2)
+                ]
             if r0 == 0 and s > 0:
                 emit(s - 1)
             rows = slice(r0, r0 + CONV_ROWS)

time: 85.3 us -> 85.3 us (level)
  no operation moved by 1% of the time
where the time goes in v4:
time: 85.3 us; the launch traced here: 84.2 us
  starting transfers between devices  39.1 us (46%)
  Pallas kernels  36.1 us (42%)
  waiting for transfers between devices  4.92 us (6%)
  local copies, waits for them, and re-layouts  3.46 us (4%)
    all_to_all x3, starting transfers between devices, exchange(): lax.all_to_all(pieces, ('seq', 'grp'), split_axis=0, concat_axis=0, tiled...  27.8 us
    pallas_call x1, Pallas kernels, intra(): pl.pallas_call(intra_kernel, grid=(GROUPS, L_DEV // BLOCK), in_specs=[pl....  11.3 us
    pallas_call x1, Pallas kernels, conv(): pl.pallas_call(conv_kernel, grid_spec=pltpu.PrefetchScalarGridSpec(num_sc...  9.44 us
    pallas_call x1, Pallas kernels, finish(): pl.pallas_call(out_kernel, grid_spec=pltpu.PrefetchScalarGridSpec(num_sca...  7.4 us
    ppermute x1, starting transfers between devices, body(): lax.ppermute(passed, 'seq', [(r, r ^ 1) for r in range(SHARDS)])  5.23 us
    ppermute x1, starting transfers between devices, body(): before = lax.ppermute(conv_input[:, L_DEV - 3:, :], 'seq', route)  4.53 us
    ppermute x1, waiting for transfers between devices, body(): lax.ppermute(passed, 'seq', [(r, r ^ 1) for r in range(SHARDS)])  3.52 us
    pallas_call x1, Pallas kernels, prep(): pl.pallas_call(prep_kernel, out_shape=(jax.ShapeDtypeStruct((HEADS, L_DEV...  2.29 us
  transfers between devices with their start and end apart: 6, of which 2 were waited for; matrix products, arithmetic and copies ran while one was open for 2% of the time, Pallas kernels for 27%

profile of v4, /device:TPU:1, one launch (start us, length us, event | category | flops | bytes accessed | tf_op | source)
XLA Modules:
  0.0 84.2 jit_solution(9325434748578349189)
XLA Ops:
  0.6 1.5 %slice.9 = bf16[1,3,5120]{2,1,0:T(4,128)(2,1)} slice(bf16[1,512,5120]{2,1,0:T(8,128)(2,1)} %c_ref.1), slice={[0:1], [509:512], [0:5120]} | slice | bytes 61440 | tf_op jit(solution)/shard_map/slice | solution.py:456
  2.2 4.5 %collective-permute-start = (bf16[1,3,5120]{2,1,0:T(4,128)(2,1)}, bf16[1,3,5120]{2,1,0:T(4,128)(2,1)}, u32[]{:S(2)}, u32[]{:S(2)}) collective-permute-start(bf16[1,3,5120]{2,1,0:T(4,128)(2,1)} %slice.9), channel_id=1, source_target_pairs={{0,16},{16,32},{32,48},{48,64},{64,80},{80,96},{96,112},{112,128},... | collective-permute-start | bytes 92168 | tf_op jit(solution)/shard_map/ppermute | solution.py:456
  6.7 2.3 %prep.1 = (f32[64,512]{1,0:T(8,128)}, f32[512,128]{1,0:T(8,128)}, bf16[4,512,128]{2,1,0:T(8,128)(2,1)}) custom-call(f32[1,64,512]{2,1,0:T(8,128)} %step_ref.1, f32[1,64]{1,0:T(1,128)} %bitcast.11), custom_call_target="tpu_custom_call" | custom-call | flops 1000000000 | bytes 2097152 | tf_op jit(solution)/shard_map/prep/pallas_call | solution.py:88
  9.0 1.3 %broadcast_in_dim.19.bx_ref.bb_ref.bc_ref = bf16[1,5120]{1,0:T(2,128)(2,1)} reshape(bf16[5120]{0:T(1024)(128)(2,1)} %param.11) | data formatting | bytes 20480 | tf_op jit(solution)/shard_map/broadcast_in_dim | solution.py:458
  10.3 0.0 collective-permute-done.hx_ref.hb_ref.hc_ref
  10.3 9.4 %conv_state.1 = (bf16[512,4096]{1,0:T(8,128)(2,1)}, bf16[512,512]{1,0:T(8,128)(2,1)}, bf16[4,128,1024]{2,1,0:T(8,128)(2,1)}, bf16[16,136,256]{2,1,0:T(8,128)(2,1)}) custom-call(s32[1]{0:T(128)S(6)} %xor.4.mask_ref, bf16[1,512,5120]{2,1,0:T(8,128)(2,1)} %c_ref.1, bf16[1,512,5120]{2,1,0:T(8,128)(2,1)} %c_ref.1, ...), custom_call_target="tpu_custom_call" | custom-call | flops 10000000000 | bytes 14680064 | tf_op jit(solution)/shard_map/conv_state/pallas_call | solution.py:194
  19.7 7.4 %all-to-all-start = ((bf16[16,136,256]{2,1,0:T(8,128)(2,1)}), bf16[16,136,256]{2,1,0:T(8,128)(2,1)}, u32[]{:S(2)}, u32[]{:S(2)}) async-start(bf16[16,136,256]{2,1,0:T(8,128)(2,1)} %get-tuple-element.21), calls=%async_computation | async-start | bytes 2228224 | tf_op jit(solution)/shard_map/all_to_all | solution.py:447
  27.2 11.3 %intra.1 = (bf16[512,4096]{1,0:T(8,128)(2,1)}, bf16[512,512]{1,0:T(8,128)(2,1)}) custom-call(bf16[512,4096]{1,0:T(8,128)(2,1)} %get-tuple-element.22.x_ref, bf16[512,512]{1,0:T(8,128)(2,1)} %get-tuple-element.23.b_ref, bf16[1,512,5120]{2,1,0:T(8,128)(2,1)} %c_ref.1, bf16[1,3,5120]{2,1,0:T(4,128)(2,1)} %collective-permute-done.hx_ref.hb_ref.hc_ref, ...), custom_call_target="tpu_custom_call" | custom-call | flops 12000000000 | bytes 12582912 | tf_op jit(solution)/shard_map/intra/pallas_call | solution.py:285
  38.5 1.4 %all-to-all-done.r_ref = bf16[16,136,256]{2,1,0:T(8,128)(2,1)} async-done(((bf16[16,136,256]{2,1,0:T(8,128)(2,1)}), bf16[16,136,256]{2,1,0:T(8,128)(2,1)}, u32[]{:S(2)}, u32[]{:S(2)}) %all-to-all-start) | async-done | bytes 1114144 | tf_op jit(solution)/shard_map/all_to_all | solution.py:447
  39.9 2.2 %scan.1 = (bf16[16,128,256]{2,1,0:T(8,128)(2,1)}, bf16[144,256]{1,0:T(8,128)(2,1)}) custom-call(bf16[16,136,256]{2,1,0:T(8,128)(2,1)} %all-to-all-done.r_ref), custom_call_target="tpu_custom_call" | custom-call | flops 1000000000 | bytes 4194304 | tf_op jit(solution)/shard_map/scan/pallas_call | solution.py:329
  42.0 8.0 %all-to-all-start.1 = ((bf16[16,128,256]{2,1,0:T(8,128)(2,1)}), bf16[16,128,256]{2,1,0:T(8,128)(2,1)}, u32[]{:S(2)}, u32[]{:S(2)}) async-start(bf16[16,128,256]{2,1,0:T(8,128)(2,1)} %get-tuple-element.31), calls=%async_computation.1 | async-start | bytes 2097152 | tf_op jit(solution)/shard_map/all_to_all | solution.py:447
  50.0 1.5 %collective-permute-start.1 = (bf16[144,256]{1,0:T(8,128)(2,1)}, bf16[144,256]{1,0:T(8,128)(2,1)S(1)}, u32[]{:S(2)}, u32[]{:S(2)}) collective-permute-start(bf16[144,256]{1,0:T(8,128)(2,1)} %get-tuple-element.32), channel_id=1, source_target_pairs={{0,0},{1,1},{2,2},{3,3},{4,4},{5,5},{6,6},{7,7},{8,8},{9,9},{10,10... | collective-permute-start | bytes 221192 | tf_op jit(solution)/shard_map/ppermute | solution.py:467
  51.6 0.0 collective-permute-done.1
  51.6 0.6 fusion
  52.2 5.2 %collective-permute-start.2 = (bf16[72,256]{1,0:T(8,128)(2,1)S(1)}, bf16[72,256]{1,0:T(8,128)(2,1)}, u32[]{:S(2)}, u32[]{:S(2)}) collective-permute-start(bf16[72,256]{1,0:T(8,128)(2,1)S(1)} %get-tuple-element.37), channel_id=1, source_target_pairs={{0,16},{16,0},{32,48},{48,32},{64,80},{80,64},{96,112},{112,96},{1... | collective-permute-start | bytes 110600 | tf_op jit(solution)/shard_map/ppermute | solution.py:469
  57.4 3.5 %collective-permute-done.2.refs_1_ = bf16[72,256]{1,0:T(8,128)(2,1)} collective-permute-done((bf16[72,256]{1,0:T(8,128)(2,1)S(1)}, bf16[72,256]{1,0:T(8,128)(2,1)}, u32[]{:S(2)}, u32[]{:S(2)}) %collective-permute-start.2) | collective-permute-done | bytes 36896 | tf_op jit(solution)/shard_map/ppermute | solution.py:469
  60.9 1.7 %pack.1 = bf16[16,72,256]{2,1,0:T(8,128)(2,1)} custom-call(s32[1]{0:T(128)} %bitcast.2.place_ref, s32[1]{0:T(128)} %bitcast.prompt_ref, s32[16]{0:T(128)} %owner_ref.3, bf16[72,256]{1,0:T(8,128)(2,1)} %get-tuple-element.38.refs_0_, bf16[72,256]{1,0:T(8,128)(2,1)} %collective-permute-done.2.refs_1_), custom_call_target="tpu_custom_call" | custom-call | flops 100000000 | bytes 524288 | tf_op jit(solution)/shard_map/pack/pallas_call | solution.py:355
  62.6 0.0 all-to-all-done.1.state_ref
  62.6 12.3 %all-to-all-start.2 = ((bf16[16,72,256]{2,1,0:T(8,128)(2,1)}), bf16[16,72,256]{2,1,0:T(8,128)(2,1)}, u32[]{:S(2)}, u32[]{:S(2)}) async-start(bf16[16,72,256]{2,1,0:T(8,128)(2,1)} %pack.1), calls=%async_computation.2 | async-start | bytes 1179648 | tf_op jit(solution)/shard_map/all_to_all | solution.py:447
  74.9 7.4 %finish.1 = bf16[1,512,4096]{2,1,0:T(8,128)(2,1)} custom-call(s32[1]{0:T(128)S(6)} %xor.4.mask_ref, bf16[512,4096]{1,0:T(8,128)(2,1)} %get-tuple-element.27.y_ref, bf16[512,512]{1,0:T(8,128)(2,1)} %get-tuple-element.28.c_ref, bf16[4,512,128]{2,1,0:T(8,128)(2,1)} %get-tuple-element.20.col_ref, bf16[4,128,1024]{2,1,0:T(8,128)(2,1)} %get-tuple-element.29.e0_ref, ...), custom_call_target="tpu_custom_call" | custom-call | flops 8000000000 | bytes 12582912 | tf_op jit(solution)/shard_map/finish/pallas_call | solution.py:422
  82.3 0.0 all-to-all-done.2.r_ref
  82.3 1.8 %unpack.1 = (f32[256,128]{1,0:T(8,128)}, bf16[4,320]{1,0:T(4,128)(2,1)}) custom-call(s32[1]{0:T(128)} %bitcast.2.place_ref, s32[1]{0:T(128)} %bitcast.prompt_ref, s32[16]{0:T(128)} %owner_ref.3, bf16[16,72,256]{2,1,0:T(8,128)(2,1)} %all-to-all-done.2.r_ref), custom_call_target="tpu_custom_call" | custom-call | flops 100000000 | bytes 524288 | tf_op jit(solution)/shard_map/unpack/pallas_call | solution.py:382
Async XLA Ops:
  2.2 8.1 %collective-permute-start = (bf16[1,3,5120]{2,1,0:T(4,128)(2,1)}, bf16[1,3,5120]{2,1,0:T(4,128)(2,1)}, u32[]{:S(2)}, u32[]{:S(2)}) collective-permute-start(bf16[1,3,5120]{2,1,0:T(4,128)(2,1)} %slice.9), channel_id=1, source_target_pairs={{0,16},{16,32},{32,48},{48,64},{64,80},{80,96},{96,112},{112,128},... | collective-permute-start | bytes 92168 | tf_op jit(solution)/shard_map/ppermute | solution.py:456
  19.7 20.1 %all-to-all-start = ((bf16[16,136,256]{2,1,0:T(8,128)(2,1)}), bf16[16,136,256]{2,1,0:T(8,128)(2,1)}, u32[]{:S(2)}, u32[]{:S(2)}) async-start(bf16[16,136,256]{2,1,0:T(8,128)(2,1)} %get-tuple-element.21), calls=%async_computation | async-start | bytes 2228224 | tf_op jit(solution)/shard_map/all_to_all | solution.py:447
  42.0 20.6 %all-to-all-start.1 = ((bf16[16,128,256]{2,1,0:T(8,128)(2,1)}), bf16[16,128,256]{2,1,0:T(8,128)(2,1)}, u32[]{:S(2)}, u32[]{:S(2)}) async-start(bf16[16,128,256]{2,1,0:T(8,128)(2,1)} %get-tuple-element.31), calls=%async_computation.1 | async-start | bytes 2097152 | tf_op jit(solution)/shard_map/all_to_all | solution.py:447
  50.0 1.5 %collective-permute-start.1 = (bf16[144,256]{1,0:T(8,128)(2,1)}, bf16[144,256]{1,0:T(8,128)(2,1)S(1)}, u32[]{:S(2)}, u32[]{:S(2)}) collective-permute-start(bf16[144,256]{1,0:T(8,128)(2,1)} %get-tuple-element.32), channel_id=1, source_target_pairs={{0,0},{1,1},{2,2},{3,3},{4,4},{5,5},{6,6},{7,7},{8,8},{9,9},{10,10... | collective-permute-start | bytes 221192 | tf_op jit(solution)/shard_map/ppermute | solution.py:467
  52.2 8.8 %collective-permute-start.2 = (bf16[72,256]{1,0:T(8,128)(2,1)S(1)}, bf16[72,256]{1,0:T(8,128)(2,1)}, u32[]{:S(2)}, u32[]{:S(2)}) collective-permute-start(bf16[72,256]{1,0:T(8,128)(2,1)S(1)} %get-tuple-element.37), channel_id=1, source_target_pairs={{0,16},{16,0},{32,48},{48,32},{64,80},{80,64},{96,112},{112,96},{1... | collective-permute-start | bytes 110600 | tf_op jit(solution)/shard_map/ppermute | solution.py:469
  62.6 19.7 %all-to-all-start.2 = ((bf16[16,72,256]{2,1,0:T(8,128)(2,1)}), bf16[16,72,256]{2,1,0:T(8,128)(2,1)}, u32[]{:S(2)}, u32[]{:S(2)}) async-start(bf16[16,72,256]{2,1,0:T(8,128)(2,1)} %pack.1), calls=%async_computation.2 | async-start | bytes 1179648 | tf_op jit(solution)/shard_map/all_to_all | solution.py:447
